TPU v7x, 128 devices: a whole 4x4x4 slice. The times are simulated.
128 devices in a mesh: gx: 8 (over z, core), gy: 16 (over x, y).
Axes of the slice: x: 4, y: 4, z: 4, core: 2. Of those that a mesh axis runs over, the one named last changes fastest.
Arguments:
- tprime: float32 [512, 512, 128], P('gx', 'gy'), may hold values from -5 to 5
- vapor: float32 [512, 512, 128], P('gx', 'gy'), may hold values from -0.2 to 0.2
- wind_u: float32 [512, 512, 128], P('gx', 'gy'), may hold values from -2.5 to 2.5
- wind_v: float32 [512, 512, 128], P('gx', 'gy'), may hold values from -2.5 to 2.5
- wind_w: float32 [512, 512, 128], P('gx', 'gy'), may hold values from -2.5 to 2.5
- radius: float32 [131072, 128], P(('gx', 'gy')), may hold values from 4 to 20
- min_radius: float32 [131072, 128], P(('gx', 'gy')), may hold values from 1 to 4
- multiplicity: float32 [131072, 128], P(('gx', 'gy')), may hold values from 0.5 to 2
- drop_counts: int32 [131072], P(('gx', 'gy')), may hold values from 0 to 128, as said below
- cell_index: int32 [131072], P(('gx', 'gy')), may hold values from 0 to 262143
- move_list: int32 [131072], P(('gx', 'gy')), may hold values from -1 to 1023, as said below
Outputs:
- temperature_out: float32 [512, 512, 128], P('gx', 'gy')
- vapor_out: float32 [512, 512, 128], P('gx', 'gy')
- radius_out: float32 [65536, 128], P(('gx', 'gy'))
- multiplicity_out: float32 [65536, 128], P(('gx', 'gy'))
Inputs may be any that keep to these rules, and one draw needn't show every extreme that they name: `move_list`: each entry is -1 for an empty home slot, else o * 8 + k: the block goes to owner o as the k-th block from its device to o. Within one device no value repeats, every owner receives exactly 512 blocks, some device holds 1024 live blocks and uses k = 7. `drop_counts`: 0 exactly in the home slots whose move_list entry is -1, else 1 to 128.
All inputs are finite; a program needn't handle non-finite values.
Results may differ from a plain program's by a relative error of at most 0.0003.
Values sent between devices are 32-bit elements; how exact they have to be, the bound alone decides.
A program may use at most 64 MiB of HBM per device.

v0:
```python
import jax
import jax.numpy as jnp
from jax import lax
from jax.experimental import pallas as pl
from jax.experimental.pallas import tpu as pltpu
from jax.sharding import PartitionSpec as P

SUBSTEPS = 6
BLK_DEV = 512


clausius = 0.07
growth = 200.0 / 3.0
solute = 0.05
condense = 5e-07
latent = 10.0
collect = 1e-07
time_step = 2.0
advect_step = 0.6


def cut_along(array, dim, size):
    before, after = (array.shape[:dim], array.shape[dim + 1 :])
    return jnp.moveaxis(array.reshape(*before, size, -1, *after), dim, 0)


def laid_out(parts, dim):
    lengths = list(parts.shape[1:])
    lengths[dim] *= parts.shape[0]
    return jnp.moveaxis(parts, 0, dim).reshape(lengths)


def exchange_both(array, axis, axes, splits, concats):
    sizes = [lax.axis_size(a) for a in axes]
    parts = cut_along(array, splits[0], sizes[0])
    parts = jnp.moveaxis(cut_along(parts, splits[1] + 1, sizes[1]), 0, 1)
    inside = parts.shape[2:]
    parts = parts.reshape(-1, *inside)
    parts = lax.all_to_all(parts, axis, split_axis=0, concat_axis=0, tiled=True)
    parts = laid_out(parts.reshape(*sizes, *inside), concats[0] + 1)
    return laid_out(parts, concats[1])


def with_halo(array, sides, width):
    edges = {}
    for axis, dim in sides:
        size, length = (lax.axis_size(axis), array.shape[dim])
        up = [(i, (i + 1) % size) for i in range(size)]
        last = lax.slice_in_dim(array, length - width, length, axis=dim)
        first = lax.slice_in_dim(array, 0, width, axis=dim)
        edges[dim] = (
            lax.ppermute(last, axis, up),
            lax.ppermute(first, axis, [(b, a) for a, b in up]),
        )
    done = []
    for _, dim in sides:
        low, high = edges[dim]
        around = [(width, width) if d in done else (0, 0) for d in range(array.ndim)]
        array = jnp.concatenate([jnp.pad(low, around), array, jnp.pad(high, around)], axis=dim)
        done.append(dim)
    return array


def batcher(n):
    out = []
    p = 1
    while p < n:
        k = p
        while k >= 1:
            for j in range(k % p, n - k, 2 * k):
                for i in range(min(k, n - j - k)):
                    if (i + j) // (2 * p) == (i + j + k) // (2 * p):
                        out.append((i + j, i + j + k))
            k //= 2
        p *= 2
    return out

NET16 = batcher(16)

def halves(top, n=16):
    out = []
    d = top
    while d >= 1:
        for i in range(n):
            if not i & d:
                out.append((i, i + d))
        d //= 2
    return out

def make_passes():
    passes = []
    up, down = list(range(16)), list(range(15, -1, -1))
    passes.append((4, [(lambda t: t * 32, up, up, NET16), (lambda t: t * 32, [16 + o for o in up], [16 + o for o in down], NET16)]))
    for level in (32, 64, 128):
        step = level // 16
        if level == 128:
            passes.append((step, [(lambda t: t, [step * o for o in up], [step * o for o in up], halves(8))]))
        else:
            per = step
            passes.append((128 // level, [(lambda t, b=b, level=level: t * level + b, [step * o for o in up], [step * o for o in up], halves(8)) for b in range(per)]))
        ces = halves(step // 2)
        if level == 128:
            passes.append((8, [(lambda t: t * 16, up, up, ces)]))
        else:
            sets = []
            for s in range(2 * level // 16):
                loads = [16 * s + o for o in up]
                stores = loads if s * 16 < level else [level + 2 * level - 1 - o for o in loads]
                sets.append((lambda t, level=level: t * 2 * level, loads, stores, ces))
            passes.append((128 // (2 * level), sets))
    return passes

PASSES = make_passes()
N_CE = sum(trips * sum(len(s[3]) for s in sets) for trips, sets in PASSES)

def moves(sets):
    return any(set(s[1]) != set(s[2]) for s in sets)

def row(ref, d):
    if isinstance(d, int):
        return ref.at[pl.ds(d * 8, 8), :]
    return ref.at[pl.ds(pl.multiple_of(d * 8, 8), 8), :]

def loop(trips, body):
    if trips == 1:
        body(0)
    else:
        def step(t, c):
            body(t)
            return c
        lax.fori_loop(0, trips, step, 0)

def sort_blocks(keys, vals, marks):
    at = 0
    side = 0
    for trips, sets in PASSES:
        count = sum(len(s[3]) for s in sets)
        key, val = keys[side], vals[side]
        if moves(sets):
            side = 1 - side
        key_to, val_to = keys[side], vals[side]
        def body(t, sets=sets, at=at, count=count, key=key, val=val, key_to=key_to, val_to=val_to):
            m = at + t * count
            for base, loads, stores, ces in sets:
                b = base(t)
                ks = [row(key, b + o)[...] for o in loads]
                vs = [row(val, b + o)[...] for o in loads]
                for i, j in ces:
                    c = ks[i] > ks[j]
                    row(marks, m)[...] = jnp.where(c, 1.0, 0.0)
                    m = m + 1
                    ks[i], ks[j] = jnp.minimum(ks[i], ks[j]), jnp.maximum(ks[i], ks[j])
                    vs[i], vs[j] = jnp.where(c, vs[j], vs[i]), jnp.where(c, vs[i], vs[j])
                for o, k, v in zip(stores, ks, vs):
                    row(key_to, b + o)[...] = k
                    row(val_to, b + o)[...] = v
        loop(trips, body)
        at += trips * count

def unsort_blocks(firsts, seconds, marks):
    at = N_CE
    side = 0
    for trips, sets in reversed(PASSES):
        count = sum(len(s[3]) for s in sets)
        at -= trips * count
        xa, xb = firsts[side], seconds[side]
        if moves(sets):
            side = 1 - side
        xa_to, xb_to = firsts[side], seconds[side]
        def body(t, sets=sets, at=at, count=count, xa=xa, xb=xb, xa_to=xa_to, xb_to=xb_to):
            m = at + t * count
            for base, loads, stores, ces in sets:
                b = base(t)
                xs = [row(xa, b + o)[...] for o in stores]
                ys = [row(xb, b + o)[...] for o in stores]
                for q in reversed(range(len(ces))):
                    i, j = ces[q]
                    c = row(marks, m + q)[...] > 0.5
                    xs[i], xs[j] = jnp.where(c, xs[j], xs[i]), jnp.where(c, xs[i], xs[j])
                    ys[i], ys[j] = jnp.where(c, ys[j], ys[i]), jnp.where(c, ys[i], ys[j])
                m = m + len(ces)
                for o, x, y in zip(loads, xs, ys):
                    row(xa_to, b + o)[...] = x
                    row(xb_to, b + o)[...] = y
        loop(trips, body)

def physics_kernel(rad_ref, flo_ref, mul_ref, cnt_ref, ct_ref, cv_ref, ro_ref, mo_ref, heat_ref, R, S, C, F, M, marks):
    def enter(g, c):
        at = pl.ds(pl.multiple_of(g * 128, 128), 128)
        to = pl.ds(g, 128, stride=8)
        R[to, :] = rad_ref[at, :].T
        F[to, :] = flo_ref[at, :].T
        M[to, :] = mul_ref[at, :].T
        return c
    lax.fori_loop(0, 8, enter, 0)
    counts = cnt_ref[...]
    zero = jnp.zeros((8, 128), jnp.float32)
    U = 8

    def init(t, w):
        for u in range(U):
            d = t * U + u
            r = row(R, d)[...]
            f = row(F, d)[...]
            m = jnp.where(counts > d, row(M, d)[...], 0.0)
            r2 = r * r
            f2 = f * f
            row(M, d)[...] = m
            row(R, d)[...] = r2
            row(S, d)[...] = lax.rsqrt(r2)
            row(F, d)[...] = f2
            row(C, d)[...] = (growth * solute) * f2 * f
            w = w + m * (r2 * r)
        return w
    weight = lax.fori_loop(0, 128 // U, init, zero)
    temp = ct_ref[...]
    wet = cv_ref[...]
    for _ in range(SUBSTEPS):
        sat = growth * ((1.0 + wet) * jnp.exp(-clausius * temp) - 1.0)
        def sub(t, w):
            for u in range(U):
                d = t * U + u
                r2 = row(R, d)[...]
                rs = row(S, d)[...]
                g = jnp.maximum(r2 + (sat + row(C, d)[...] * (rs * rs * rs)), row(F, d)[...])
                ns = lax.rsqrt(g)
                row(R, d)[...] = g
                row(S, d)[...] = ns
                w = w + row(M, d)[...] * (g * (g * ns))
            return w
        after = lax.fori_loop(0, 128 // U, sub, zero)
        condensed = after - weight
        weight = after
        wet = wet - condense * condensed
        temp = temp + latent * condense * condensed
    heat_ref[0] = temp - ct_ref[...]
    heat_ref[1] = wet - cv_ref[...]

    def radii(t, c):
        for u in range(U):
            d = t * U + u
            row(R, d)[...] = row(R, d)[...] * row(S, d)[...]
        return c
    lax.fori_loop(0, 128 // U, radii, 0)
    sort_blocks((R, S), (M, C), marks)

    def both(t, carry):
        a0, a1, a3, a4, b0, b1, b3, b4 = carry
        for u in range(U):
            d = t * U + u
            r = row(R, d)[...]
            m = row(M, d)[...]
            r2 = r * r
            r3 = r2 * r
            r4 = r2 * r2
            gain = r4 * a0 + 2.0 * (r3 * a1 - r * a3) - a4
            w = m * r3
            a0 = a0 + w
            a1 = a1 + w * r
            a3 = a3 + w * r3
            a4 = a4 + w * r4
            grown = r3 + (time_step * collect) * gain
            row(S, d)[...] = jnp.where(m > 0.0, jnp.exp(jnp.log(grown) * (1.0 / 3.0)), 0.0)
            d = 127 - d
            r = row(R, d)[...]
            m = row(M, d)[...]
            r2 = r * r
            r3 = r2 * r
            r4 = r2 * r2
            loss = b4 + 2.0 * (r * b3 - r3 * b1) - r4 * b0
            b0 = b0 + m
            b1 = b1 + m * r
            b3 = b3 + m * r3
            b4 = b4 + m * r4
            row(C, d)[...] = m * jnp.exp((-time_step * collect) * loss)
        return a0, a1, a3, a4, b0, b1, b3, b4
    lax.fori_loop(0, 128 // U, both, (zero,) * 8)
    unsort_blocks((S, R), (C, F), marks)

    def leave(g, c):
        at = pl.ds(pl.multiple_of(g * 128, 128), 128)
        frm = pl.ds(g, 128, stride=8)
        ro_ref[at, :] = S[frm, :].T
        mo_ref[at, :] = C[frm, :].T
        return c
    lax.fori_loop(0, 8, leave, 0)

def physics(radius, floor_radius, mult, counts, cell_temp, cell_vapor):
    f32 = jnp.float32
    return pl.pallas_call(
        physics_kernel,
        out_shape=(jax.ShapeDtypeStruct((1024, 128), f32), jax.ShapeDtypeStruct((1024, 128), f32), jax.ShapeDtypeStruct((2, 8, 128), f32)),
        in_specs=[pl.BlockSpec(memory_space=pltpu.VMEM)] * 6,
        out_specs=[pl.BlockSpec(memory_space=pltpu.VMEM)] * 3,
        scratch_shapes=[pltpu.VMEM((1024, 128), f32)] * 5 + [pltpu.VMEM((N_CE * 8, 128), f32)],
        compiler_params=pltpu.CompilerParams(vmem_limit_bytes=40 * 2**20),
        cost_estimate=pl.CostEstimate(flops=30_000_000, bytes_accessed=3_000_000, transcendentals=1_000_000),
        name="physics",
    )(radius, floor_radius, mult, counts, cell_temp, cell_vapor)


def tendency(padded, along_x, along_y, along_z):
    middle_y = padded[:, :, 1:-1]
    flux_x = along_x * (0.5 * (middle_y[:, :-1] + middle_y[:, 1:]))
    middle_x = padded[:, 1:-1]
    flux_y = along_y * (0.5 * (middle_x[:, :, :-1] + middle_x[:, :, 1:]))
    core = padded[:, 1:-1, 1:-1]
    flux_z = along_z * (0.5 * (core[..., :-1] + core[..., 1:]))
    edge = jnp.zeros(core.shape[:-1] + (1,), core.dtype)
    flux_z = jnp.concatenate([edge, flux_z, edge], axis=-1)
    return (
        -(flux_x[:, 1:] - flux_x[:, :-1])
        - (flux_y[:, :, 1:] - flux_y[:, :, :-1])
        - (flux_z[..., 1:] - flux_z[..., :-1])
    )


def selector(index, count):
    return (jnp.arange(count, dtype=jnp.int32)[:, None] == index[None, :]).astype(jnp.float32)


def select_rows(matrix, value):
    flat = value.reshape((value.shape[0], -1))
    picked = jnp.dot(
        matrix, flat, precision=lax.Precision.HIGHEST, preferred_element_type=jnp.float32
    )
    return picked.reshape((matrix.shape[0],) + value.shape[1:])


def select_back(matrix, value):
    picked = lax.dot_general(
        matrix,
        value,
        (((0,), (0,)), ((), ())),
        precision=lax.Precision.HIGHEST,
        preferred_element_type=jnp.float32,
    )
    return picked


def single(value, cap):
    lead = (lax.axis_size("gx"), lax.axis_size("gy"), cap)
    moved = exchange_both(
        value.reshape(lead + value.shape[1:]), ("gx", "gy"), ("gx", "gy"), (0, 1), (0, 1)
    )
    return moved.reshape(value.shape)


def compact(taken):
    position = jnp.cumsum(taken.astype(jnp.int32)) - 1
    target = jnp.where(taken, position, BLK_DEV)
    return selector(target, BLK_DEV)


def advance(state):
    padded = with_halo(state, (("gx", 1), ("gy", 2)), 1)
    return padded


def body(
    tprime,
    vapor,
    wind_u,
    wind_v,
    wind_w,
    radius,
    min_radius,
    multiplicity,
    drop_counts,
    cell_index,
    move_list,
):
    devices = lax.axis_size("gx") * lax.axis_size("gy")
    home = radius.shape[0]
    drops = radius.shape[1]
    cap = (home + devices - 1) // devices
    slots = devices * cap
    columns = tprime.shape[0] * tprime.shape[1]
    levels = tprime.shape[2]
    live = move_list >= 0
    target = jnp.where(live, move_list, slots)
    placing = selector(target, slots)
    column_pick = selector(cell_index // levels, columns).T
    level_pick = selector(cell_index % levels, levels).T
    fields = jnp.concatenate(
        [tprime.reshape(columns, levels), vapor.reshape(columns, levels)], axis=1
    )
    at_column = select_rows(column_pick, fields)
    cell_temp = jnp.sum(at_column[:, :levels] * level_pick, axis=1)
    cell_vapor = jnp.sum(at_column[:, levels:] * level_pick, axis=1)
    square = (8, home // 8)
    radius_new, mult_new, heat = physics(
        radius,
        min_radius,
        multiplicity,
        drop_counts.reshape(square),
        cell_temp.reshape(square),
        cell_vapor.reshape(square),
    )
    bulk = single(select_rows(placing, jnp.concatenate([radius_new, mult_new], axis=1)), cap)
    gather_rows = compact(bulk[:, drops] > 0.0)
    picked = select_rows(gather_rows, bulk)
    radius_out = picked[:, :drops]
    multiplicity_out = picked[:, drops:]
    heat_t = heat[0].reshape(home)
    heat_v = heat[1].reshape(home)
    weighted = jnp.concatenate([level_pick * heat_t[:, None], level_pick * heat_v[:, None]], axis=1)
    added = select_back(column_pick, weighted)
    heated_t = (fields[:, :levels] + added[:, :levels]).reshape(tprime.shape)
    heated_v = (fields[:, levels:] + added[:, levels:]).reshape(vapor.shape)
    winds = with_halo(jnp.stack([wind_u, wind_v]), (("gx", 1), ("gy", 2)), 1)
    along_x = 0.5 * (winds[0, :-1, 1:-1] + winds[0, 1:, 1:-1])
    along_y = 0.5 * (winds[1, 1:-1, :-1] + winds[1, 1:-1, 1:])
    along_z = 0.5 * (wind_w[..., :-1] + wind_w[..., 1:])
    start = jnp.stack([heated_t, heated_v])
    section = start
    for weight in (1.0 / 3.0, 0.5, 1.0):
        section = start + advect_step * weight * tendency(
            advance(section), along_x, along_y, along_z
        )
    return (section[0], section[1], radius_out, multiplicity_out)


def solution(mesh):
    placed = (
        P("gx", "gy", None),
        P("gx", "gy", None),
        P("gx", "gy", None),
        P("gx", "gy", None),
        P("gx", "gy", None),
        P(("gx", "gy"), None),
        P(("gx", "gy"), None),
        P(("gx", "gy"), None),
        P(("gx", "gy")),
        P(("gx", "gy")),
        P(("gx", "gy")),
    )
    return jax.shard_map(
        body,
        mesh=mesh,
        in_specs=placed,
        out_specs=(
            P("gx", "gy", None),
            P("gx", "gy", None),
            P(("gx", "gy"), None),
            P(("gx", "gy"), None),
        ),
        check_vma=False,
    )
```

profile of v0, /device:TPU:0, one launch (start us, length us, event | category | flops | bytes accessed | tf_op | source)
XLA Modules:
  0.0 95.2 jit_solution(5891658544332424295)
XLA Ops:
  0.7 1.5 %pad_maximum_fusion.28 = (f32[2,1,32,128]{3,2,1,0:T(8,128)}, f32[2,1,32,128]{3,2,1,0:T(8,128)S(1)}) fusion(f32[1,64,32,128]{3,2,1,0:T(8,128)} %bitcast.60, f32[1,64,32,128]{3,2,1,0:T(8,128)} %bitcast.64), kind=kLoop, calls=%fused_computation.146 | loop fusion | flops 16384 | bytes 2162688 | tf_op jit(solution)/shard_map/slice | solution.py:49
  2.2 3.6 %collective-permute-start.3 = (f32[2,1,32,128]{3,2,1,0:T(8,128)S(1)}, f32[2,1,32,128]{3,2,1,0:T(8,128)S(1)}, u32[]{:S(2)}, u32[]{:S(2)}) collective-permute-start(f32[2,1,32,128]{3,2,1,0:T(8,128)S(1)} %get-tuple-element.27), channel_id=1, source_target_pairs={{16,0},{32,16},{48,32},{64,48},{80,64},{96,80},{112,96},{0,112},{1... | collective-permute-start | bytes 98312 | tf_op jit(solution)/shard_map/ppermute | solution.py:53
  5.8 0.1 pad_maximum_fusion.26
  5.9 1.6 %collective-permute-start.6 = (f32[2,64,1,128]{3,2,1,0:T(1,128)S(1)}, f32[2,64,1,128]{3,2,1,0:T(1,128)S(1)}, u32[]{:S(2)}, u32[]{:S(2)}) collective-permute-start(f32[2,64,1,128]{3,2,1,0:T(1,128)S(1)} %get-tuple-element.24), channel_id=1, source_target_pairs={{0,1},{1,2},{2,3},{3,4},{4,5},{5,6},{6,7},{7,8},{8,9},{9,10},{10,1... | collective-permute-start | bytes 196616 | tf_op jit(solution)/shard_map/ppermute | solution.py:52
  7.6 3.8 %collective-permute-start.7 = (f32[2,64,1,128]{3,2,1,0:T(1,128)S(1)}, f32[2,64,1,128]{3,2,1,0:T(1,128)S(1)}, u32[]{:S(2)}, u32[]{:S(2)}) collective-permute-start(f32[2,64,1,128]{3,2,1,0:T(1,128)S(1)} %get-tuple-element.25), channel_id=1, source_target_pairs={{1,0},{2,1},{3,2},{4,3},{5,4},{6,5},{7,6},{8,7},{9,8},{10,9},{11,1... | collective-permute-start | bytes 196616 | tf_op jit(solution)/shard_map/ppermute | solution.py:53
  11.4 4.2 %fusion.1 = f32[1024,256]{0,1:T(8,128)S(1)} fusion(s32[1024]{0:T(1024)S(1)} %get-tuple-element.41, f32[2048,128]{1,0:T(8,128)S(1)} %bitcast.68, f32[2048,128]{1,0:T(8,128)S(1)} %bitcast.69), kind=kOutput, calls=%fused_computation.2 | convolution fusion | flops 6445072384 | bytes 3149824 | tf_op jit(solution)/shard_map/dot_general | solution.py:324
  15.6 0.1 fusion.62
  15.8 9.5 %physics.1 = (f32[1024,128]{1,0:T(8,128)S(1)}, f32[1024,128]{1,0:T(8,128)S(1)}, f32[2,8,128]{2,1,0:T(8,128)S(1)}) custom-call(f32[1024,128]{1,0:T(8,128)S(1)} %copy-done, f32[1024,128]{1,0:T(8,128)S(1)} %copy-done.1, f32[1024,128]{1,0:T(8,128)S(1)} %copy-done.2, s32[8,128]{1,0:T(8,128)S(1)} %bitcast.43, f32[8,128]{1,0:T(8,128)S(1)} %bitcast.42, ...), custom_call_target="tpu_custom_call" | custom-call | flops 30000000 | bytes 3000000 | tf_op jit(solution)/shard_map/physics/pallas_call | solution.py:290
  25.3 0.1 fusion.65
  25.4 4.2 %fusion = f32[2048,256]{1,0:T(8,128)S(1)} fusion(s32[1024]{0:T(1024)S(1)} %get-tuple-element.41, f32[1024,128]{0,1:T(8,128)S(1)} %get-tuple-element.39, f32[1024,128]{0,1:T(8,128)S(1)} %get-tuple-element.38), kind=kOutput, calls=%fused_computation.1 | convolution fusion | flops 6444810240 | bytes 3149824 | tf_op jit(solution)/shard_map/dot_general | solution.py:331
  29.6 0.3 slice_add_fusion.2
  30.0 0.6 fusion.68
  30.6 3.1 %fusion.46 = f32[128,1,1,8,256]{4,3,2,1,0:T(8,128)} fusion(s32[1024]{0:T(1024)S(1)} %compare_select_fusion, f32[1024,128]{1,0:T(8,128)S(1)} %get-tuple-element.9, f32[1024,128]{1,0:T(8,128)S(1)} %get-tuple-element.8), kind=kOutput, calls=%fused_computation.95 | convolution fusion | flops 3222536192 | bytes 2101248 | tf_op jit(solution)/shard_map/dot_general | solution.py:324
  33.7 7.7 %all-to-all-start = ((f32[128,1,1,8,256]{4,3,2,1,0:T(8,128)}), f32[128,1,1,8,256]{4,3,2,1,0:T(8,128)}, u32[]{:S(2)}, u32[]{:S(2)}) async-start(f32[128,1,1,8,256]{4,3,2,1,0:T(8,128)} %fusion.46), calls=%async_computation | async-start | bytes 2097152 | tf_op jit(solution)/shard_map/all_to_all | solution.py:39
  41.4 1.9 %add_multiply_fusion = f32[64,32,127]{2,1,0:T(8,128)S(1)} fusion(f32[64,32,128]{2,1,0:T(8,128)} %param.15), kind=kLoop, calls=%fused_computation.129 | loop fusion | flops 520192 | bytes 3121152 | tf_op jit(solution)/shard_map/mul | solution.py:308
  43.3 0.6 fusion.22
  44.0 0.1 fusion.66
  44.1 0.6 copy-done.9
  44.7 2.5 %collective-permute-start.1 = (f32[2,1,32,128]{3,2,1,0:T(8,128)S(1)}, f32[2,1,32,128]{3,2,1,0:T(8,128)S(1)}, u32[]{:S(2)}, u32[]{:S(2)}) collective-permute-start(f32[2,1,32,128]{3,2,1,0:T(8,128)S(1)} %copy-done.9), channel_id=1, source_target_pairs={{16,0},{32,16},{48,32},{64,48},{80,64},{96,80},{112,96},{0,112},{1... | collective-permute-start | bytes 98312 | tf_op jit(solution)/shard_map/ppermute | solution.py:53
  47.2 1.5 %collective-permute-start.4 = (f32[2,64,1,128]{3,2,1,0:T(1,128)S(1)}, f32[2,64,1,128]{3,2,1,0:T(1,128)S(1)}, u32[]{:S(2)}, u32[]{:S(2)}) collective-permute-start(f32[2,64,1,128]{3,2,1,0:T(1,128)S(1)} %get-tuple-element.28), channel_id=1, source_target_pairs={{0,1},{1,2},{2,3},{3,4},{4,5},{5,6},{6,7},{7,8},{8,9},{9,10},{10,1... | collective-permute-start | bytes 196616 | tf_op jit(solution)/shard_map/ppermute | solution.py:52
  48.7 0.1 fusion.54
  48.9 3.9 %collective-permute-start.5 = (f32[2,64,1,128]{3,2,1,0:T(1,128)S(1)}, f32[2,64,1,128]{3,2,1,0:T(1,128)S(1)}, u32[]{:S(2)}, u32[]{:S(2)}) collective-permute-start(f32[2,64,1,128]{3,2,1,0:T(1,128)S(1)} %get-tuple-element.29), channel_id=1, source_target_pairs={{1,0},{2,1},{3,2},{4,3},{5,4},{6,5},{7,6},{8,7},{9,8},{10,9},{11,1... | collective-permute-start | bytes 196616 | tf_op jit(solution)/shard_map/ppermute | solution.py:53
  52.8 0.4 fusion.17
  53.2 0.2 fusion.50
  53.4 4.8 %collective-permute-done.4 = f32[2,64,1,128]{3,2,1,0:T(1,128)S(1)} collective-permute-done((f32[2,64,1,128]{3,2,1,0:T(1,128)S(1)}, f32[2,64,1,128]{3,2,1,0:T(1,128)S(1)}, u32[]{:S(2)}, u32[]{:S(2)}) %collective-permute-start.4) | collective-permute-done | bytes 65568 | tf_op jit(solution)/shard_map/ppermute | solution.py:52
  58.2 1.2 %fusion.15 = f32[2,64,33,128]{3,2,1,0:T(8,128)S(1)} fusion(f32[2,64,1,128]{3,2,1,0:T(1,128)S(1)} %collective-permute-done.5, f32[2,1,32,128]{3,2,1,0:T(8,128)S(1)} %collective-permute-done.1, f32[2,1,32,128]{3,2,1,0:T(8,128)S(1)} %collective-permute-done, f32[1,64,32,128]{3,2,1,0:T(8,128)S(1)} %bitcast.48, f32[1,64,32,128]{3,2,1,0:T(8,128)S(1)} %bitcast.56, ...), kind=kLoop, calls=%fused_computation.43 | loop fusion | flops 7569408 | bytes 5537792 | tf_op jit(solution)/shard_map/mul | solution.py:306
  59.4 1.3 %fusion.39 = f32[2,64,32,128]{3,2,1,0:T(8,128)S(1)} fusion(f32[2,64,33,128]{3,2,1,0:T(8,128)S(1)} %fusion.15, f32[2,65,32,128]{3,2,1,0:T(8,128)S(1)} %fusion.17, f32[2,64,32,127]{3,2,1,0:T(8,128)S(1)} %fusion.22, f32[1,64,32,128]{3,2,1,0:T(8,128)S(1)} %bitcast.49, f32[1,64,32,128]{3,2,1,0:T(8,128)S(1)} %bitcast.57), kind=kLoop, calls=%fused_computation.86 | loop fusion | flops 4718592 | bytes 14663680 | tf_op jit(solution)/shard_map/add | solution.py:418
  60.7 0.6 fusion.30
  61.4 2.9 %collective-permute-start.9 = (f32[2,1,32,128]{3,2,1,0:T(8,128)S(1)}, f32[2,1,32,128]{3,2,1,0:T(8,128)S(1)}, u32[]{:S(2)}, u32[]{:S(2)}) collective-permute-start(f32[2,1,32,128]{3,2,1,0:T(8,128)S(1)} %get-tuple-element.23), channel_id=1, source_target_pairs={{16,0},{32,16},{48,32},{64,48},{80,64},{96,80},{112,96},{0,112},{1... | collective-permute-start | bytes 98312 | tf_op jit(solution)/shard_map/ppermute | solution.py:53
  64.5 5.3 %collective-permute-start.11 = (f32[2,64,1,128]{3,2,1,0:T(1,128)S(1)}, f32[2,64,1,128]{3,2,1,0:T(1,128)S(1)}, u32[]{:S(2)}, u32[]{:S(2)}) collective-permute-start(f32[2,64,1,128]{3,2,1,0:T(1,128)S(1)} %get-tuple-element.21), channel_id=1, source_target_pairs={{1,0},{2,1},{3,2},{4,3},{5,4},{6,5},{7,6},{8,7},{9,8},{10,9},{11,1... | collective-permute-start | bytes 196616 | tf_op jit(solution)/shard_map/ppermute | solution.py:53
  69.8 0.4 fusion.18
  70.2 1.8 %collective-permute-done.10 = f32[2,64,1,128]{3,2,1,0:T(1,128)S(1)} collective-permute-done((f32[2,64,1,128]{3,2,1,0:T(1,128)S(1)}, f32[2,64,1,128]{3,2,1,0:T(1,128)S(1)}, u32[]{:S(2)}, u32[]{:S(2)}) %collective-permute-start.10) | collective-permute-done | bytes 65568 | tf_op jit(solution)/shard_map/ppermute | solution.py:52
  72.1 1.2 %fusion.11 = f32[2,64,33,128]{3,2,1,0:T(8,128)S(1)} fusion(f32[2,64,1,128]{3,2,1,0:T(1,128)S(1)} %collective-permute-done.11, f32[2,1,32,128]{3,2,1,0:T(8,128)S(1)} %collective-permute-done.9, f32[2,64,32,128]{3,2,1,0:T(8,128)S(1)} %fusion.39, f32[2,1,32,128]{3,2,1,0:T(8,128)S(1)} %collective-permute-done.8, ...), kind=kLoop, calls=%fused_computation.33 | loop fusion | flops 6488064 | bytes 5537792 | tf_op jit(solution)/shard_map/mul | solution.py:306
  73.3 1.3 %fusion.34 = f32[2,64,32,128]{3,2,1,0:T(8,128)S(1)} fusion(f32[2,64,33,128]{3,2,1,0:T(8,128)S(1)} %fusion.11, f32[2,65,32,128]{3,2,1,0:T(8,128)S(1)} %fusion.18, f32[2,64,32,127]{3,2,1,0:T(8,128)S(1)} %fusion.30, f32[1,64,32,128]{3,2,1,0:T(8,128)S(1)} %bitcast.50, f32[1,64,32,128]{3,2,1,0:T(8,128)S(1)} %bitcast.58), kind=kLoop, calls=%fused_computation.79 | loop fusion | flops 4718592 | bytes 14663680 | tf_op jit(solution)/shard_map/add | solution.py:418
  74.6 0.6 fusion.24
  75.2 2.9 %collective-permute-start.13 = (f32[2,1,32,128]{3,2,1,0:T(8,128)S(1)}, f32[2,1,32,128]{3,2,1,0:T(8,128)S(1)}, u32[]{:S(2)}, u32[]{:S(2)}) collective-permute-start(f32[2,1,32,128]{3,2,1,0:T(8,128)S(1)} %get-tuple-element.19), channel_id=1, source_target_pairs={{16,0},{32,16},{48,32},{64,48},{80,64},{96,80},{112,96},{0,112},{1... | collective-permute-start | bytes 98312 | tf_op jit(solution)/shard_map/ppermute | solution.py:53
  78.4 5.4 %collective-permute-start.15 = (f32[2,64,1,128]{3,2,1,0:T(1,128)S(1)}, f32[2,64,1,128]{3,2,1,0:T(1,128)S(1)}, u32[]{:S(2)}, u32[]{:S(2)}) collective-permute-start(f32[2,64,1,128]{3,2,1,0:T(1,128)S(1)} %get-tuple-element.17), channel_id=1, source_target_pairs={{1,0},{2,1},{3,2},{4,3},{5,4},{6,5},{7,6},{8,7},{9,8},{10,9},{11,1... | collective-permute-start | bytes 196616 | tf_op jit(solution)/shard_map/ppermute | solution.py:53
  83.8 0.4 fusion.19
  84.2 1.8 %collective-permute-done.14 = f32[2,64,1,128]{3,2,1,0:T(1,128)S(1)} collective-permute-done((f32[2,64,1,128]{3,2,1,0:T(1,128)S(1)}, f32[2,64,1,128]{3,2,1,0:T(1,128)S(1)}, u32[]{:S(2)}, u32[]{:S(2)}) %collective-permute-start.14) | collective-permute-done | bytes 65568 | tf_op jit(solution)/shard_map/ppermute | solution.py:52
  85.9 1.2 %fusion.7 = f32[2,64,33,128]{3,2,1,0:T(8,128)S(1)} fusion(f32[2,64,1,128]{3,2,1,0:T(1,128)S(1)} %collective-permute-done.15, f32[2,1,32,128]{3,2,1,0:T(8,128)S(1)} %collective-permute-done.13, f32[2,64,32,128]{3,2,1,0:T(8,128)S(1)} %fusion.34, f32[2,1,32,128]{3,2,1,0:T(8,128)S(1)} %collective-permute-done.12, ...), kind=kLoop, calls=%fused_computation.23 | loop fusion | flops 6488064 | bytes 5537792 | tf_op jit(solution)/shard_map/mul | solution.py:306
  87.1 1.3 %fusion.28 = f32[2,64,32,128]{3,2,1,0:T(8,128)S(1)} fusion(f32[2,64,33,128]{3,2,1,0:T(8,128)S(1)} %fusion.7, f32[2,65,32,128]{3,2,1,0:T(8,128)S(1)} %fusion.19, f32[2,64,32,127]{3,2,1,0:T(8,128)S(1)} %fusion.24, f32[1,64,32,128]{3,2,1,0:T(8,128)S(1)} %bitcast.51, f32[1,64,32,128]{3,2,1,0:T(8,128)S(1)} %bitcast.59), kind=kLoop, calls=%fused_computation.70 | loop fusion | flops 4718592 | bytes 14663680 | tf_op jit(solution)/shard_map/add | solution.py:418
  88.4 1.5 %slice_bitcast_fusion = (f32[64,32,128]{2,1,0:T(8,128)}, f32[64,32,128]{2,1,0:T(8,128)}) fusion(f32[2,64,32,128]{3,2,1,0:T(8,128)S(1)} %fusion.28), kind=kLoop, calls=%fused_computation.118 | loop fusion | bytes 4194304 | tf_op jit(solution)/shard_map/squeeze | solution.py:421
  89.9 1.2 %convert_reduce_fusion = (s32[1024]{0:T(1024)S(1)}, pred[1024,1]{1,0:T(8,128)(4,1)S(1)}) fusion(f32[1024,256]{1,0:T(8,128)} %bitcast.21), kind=kLoop, calls=%fused_computation.135 | loop fusion | flops 2048 | bytes 9216 | tf_op jit(solution)/shard_map/convert_element_type | solution.py:350
  91.1 0.3 reduce-window.9
  91.5 0.1 slice_reduce_fusion
  91.6 0.2 reduce
  91.9 2.5 %fusion.45 = f32[512,256]{1,0:T(8,128)S(1)} fusion(s32[1024]{0:T(1024)S(1)} %bitcast_select_fusion, f32[128,1,1,8,256]{4,3,2,1,0:T(8,128)} %all-to-all-done), kind=kOutput, calls=%fused_computation.94 | convolution fusion | flops 1611137024 | bytes 1576960 | tf_op jit(solution)/shard_map/dot_general | solution.py:324
  94.4 0.8 fusion.80
  (53 shorter events, 0.7 us)
Async XLA Ops:
  0.6 5.2 %copy-start.4 = (f32[64,32,128]{2,1,0:T(8,128)S(1)}, f32[64,32,128]{2,1,0:T(8,128)}, u32[]{:S(2)}) copy-start(f32[64,32,128]{2,1,0:T(8,128)} %param.14) | copy-start | bytes 3145732
  0.6 5.2 %copy-start.5 = (f32[64,32,128]{2,1,0:T(8,128)S(1)}, f32[64,32,128]{2,1,0:T(8,128)}, u32[]{:S(2)}) copy-start(f32[64,32,128]{2,1,0:T(8,128)} %param.13) | copy-start | bytes 3145732
  0.7 10.7 %copy-start.10 = (s32[1024]{0:T(1024)S(1)}, s32[1024]{0:T(1024)}, u32[]{:S(2)}) copy-start(s32[1024]{0:T(1024)} %param.20) | copy-start | bytes 12292
  0.7 10.7 %copy-start.7 = (f32[64,32,128]{2,1,0:T(8,128)S(1)}, f32[64,32,128]{2,1,0:T(8,128)}, u32[]{:S(2)}) copy-start(f32[64,32,128]{2,1,0:T(8,128)} %param.12) | copy-start | bytes 3145732
  0.7 10.7 %copy-start.8 = (f32[64,32,128]{2,1,0:T(8,128)S(1)}, f32[64,32,128]{2,1,0:T(8,128)}, u32[]{:S(2)}) copy-start(f32[64,32,128]{2,1,0:T(8,128)} %param.11) | copy-start | bytes 3145732
  2.2 41.9 %collective-permute-start.2 = (f32[2,1,32,128]{3,2,1,0:T(8,128)}, f32[2,1,32,128]{3,2,1,0:T(8,128)S(1)}, u32[]{:S(2)}, u32[]{:S(2)}) collective-permute-start(f32[2,1,32,128]{3,2,1,0:T(8,128)} %get-tuple-element.26), channel_id=1, source_target_pairs={{0,16},{16,32},{32,48},{48,64},{64,80},{80,96},{96,112},{112,0},{1... | collective-permute-start | bytes 98312 | tf_op jit(solution)/shard_map/ppermute | solution.py:52
  2.2 45.0 %collective-permute-start.3 = (f32[2,1,32,128]{3,2,1,0:T(8,128)S(1)}, f32[2,1,32,128]{3,2,1,0:T(8,128)S(1)}, u32[]{:S(2)}, u32[]{:S(2)}) collective-permute-start(f32[2,1,32,128]{3,2,1,0:T(8,128)S(1)} %get-tuple-element.27), channel_id=1, source_target_pairs={{16,0},{32,16},{48,32},{64,48},{80,64},{96,80},{112,96},{0,112},{1... | collective-permute-start | bytes 98312 | tf_op jit(solution)/shard_map/ppermute | solution.py:53
  5.9 47.2 %collective-permute-start.6 = (f32[2,64,1,128]{3,2,1,0:T(1,128)S(1)}, f32[2,64,1,128]{3,2,1,0:T(1,128)S(1)}, u32[]{:S(2)}, u32[]{:S(2)}) collective-permute-start(f32[2,64,1,128]{3,2,1,0:T(1,128)S(1)} %get-tuple-element.24), channel_id=1, source_target_pairs={{0,1},{1,2},{2,3},{3,4},{4,5},{5,6},{6,7},{7,8},{8,9},{9,10},{10,1... | collective-permute-start | bytes 196616 | tf_op jit(solution)/shard_map/ppermute | solution.py:52
  7.6 45.6 %collective-permute-start.7 = (f32[2,64,1,128]{3,2,1,0:T(1,128)S(1)}, f32[2,64,1,128]{3,2,1,0:T(1,128)S(1)}, u32[]{:S(2)}, u32[]{:S(2)}) collective-permute-start(f32[2,64,1,128]{3,2,1,0:T(1,128)S(1)} %get-tuple-element.25), channel_id=1, source_target_pairs={{1,0},{2,1},{3,2},{4,3},{5,4},{6,5},{7,6},{8,7},{9,8},{10,9},{11,1... | collective-permute-start | bytes 196616 | tf_op jit(solution)/shard_map/ppermute | solution.py:53
  11.4 4.4 %copy-start = (f32[1024,128]{1,0:T(8,128)S(1)}, f32[1024,128]{1,0:T(8,128)}, u32[]{:S(2)}) copy-start(f32[1024,128]{1,0:T(8,128)} %rad_ref.1) | copy-start | bytes 1572868
  11.4 4.4 %copy-start.1 = (f32[1024,128]{1,0:T(8,128)S(1)}, f32[1024,128]{1,0:T(8,128)}, u32[]{:S(2)}) copy-start(f32[1024,128]{1,0:T(8,128)} %flo_ref.1) | copy-start | bytes 1572868
  11.4 4.4 %copy-start.2 = (f32[1024,128]{1,0:T(8,128)S(1)}, f32[1024,128]{1,0:T(8,128)}, u32[]{:S(2)}) copy-start(f32[1024,128]{1,0:T(8,128)} %mul_ref.1) | copy-start | bytes 1572868
  11.4 4.4 %copy-start.3 = (s32[1024]{0:T(1024)S(1)}, s32[1024]{0:T(1024)}, u32[]{:S(2)}) copy-start(s32[1024]{0:T(1024)} %param.19) | copy-start | bytes 12292
  29.9 0.7 copy-start.11
  30.6 18.3 %collective-permute-start = (f32[2,1,32,128]{3,2,1,0:T(8,128)}, f32[2,1,32,128]{3,2,1,0:T(8,128)S(1)}, u32[]{:S(2)}, u32[]{:S(2)}) collective-permute-start(f32[2,1,32,128]{3,2,1,0:T(8,128)} %get-tuple-element.30), channel_id=1, source_target_pairs={{0,16},{16,32},{32,48},{48,64},{64,80},{80,96},{96,112},{112,0},{1... | collective-permute-start | bytes 98312 | tf_op jit(solution)/shard_map/ppermute | solution.py:52
  33.7 56.2 %all-to-all-start = ((f32[128,1,1,8,256]{4,3,2,1,0:T(8,128)}), f32[128,1,1,8,256]{4,3,2,1,0:T(8,128)}, u32[]{:S(2)}, u32[]{:S(2)}) async-start(f32[128,1,1,8,256]{4,3,2,1,0:T(8,128)} %fusion.46), calls=%async_computation | async-start | bytes 2097152 | tf_op jit(solution)/shard_map/all_to_all | solution.py:39
  43.9 0.8 copy-start.9
  44.0 4.8 %copy-start.6 = (f32[64,32,128]{2,1,0:T(8,128)S(1)}, f32[64,32,128]{2,1,0:T(8,128)}, u32[]{:S(2)}) copy-start(f32[64,32,128]{2,1,0:T(8,128)} %param.13) | copy-start | bytes 3145732
  44.7 8.0 %collective-permute-start.1 = (f32[2,1,32,128]{3,2,1,0:T(8,128)S(1)}, f32[2,1,32,128]{3,2,1,0:T(8,128)S(1)}, u32[]{:S(2)}, u32[]{:S(2)}) collective-permute-start(f32[2,1,32,128]{3,2,1,0:T(8,128)S(1)} %copy-done.9), channel_id=1, source_target_pairs={{16,0},{32,16},{48,32},{64,48},{80,64},{96,80},{112,96},{0,112},{1... | collective-permute-start | bytes 98312 | tf_op jit(solution)/shard_map/ppermute | solution.py:53
  47.2 11.0 %collective-permute-start.4 = (f32[2,64,1,128]{3,2,1,0:T(1,128)S(1)}, f32[2,64,1,128]{3,2,1,0:T(1,128)S(1)}, u32[]{:S(2)}, u32[]{:S(2)}) collective-permute-start(f32[2,64,1,128]{3,2,1,0:T(1,128)S(1)} %get-tuple-element.28), channel_id=1, source_target_pairs={{0,1},{1,2},{2,3},{3,4},{4,5},{5,6},{6,7},{7,8},{8,9},{9,10},{10,1... | collective-permute-start | bytes 196616 | tf_op jit(solution)/shard_map/ppermute | solution.py:52
  48.9 9.3 %collective-permute-start.5 = (f32[2,64,1,128]{3,2,1,0:T(1,128)S(1)}, f32[2,64,1,128]{3,2,1,0:T(1,128)S(1)}, u32[]{:S(2)}, u32[]{:S(2)}) collective-permute-start(f32[2,64,1,128]{3,2,1,0:T(1,128)S(1)} %get-tuple-element.29), channel_id=1, source_target_pairs={{1,0},{2,1},{3,2},{4,3},{5,4},{6,5},{7,6},{8,7},{9,8},{10,9},{11,1... | collective-permute-start | bytes 196616 | tf_op jit(solution)/shard_map/ppermute | solution.py:53
  61.4 8.5 %collective-permute-start.8 = (f32[2,1,32,128]{3,2,1,0:T(8,128)S(1)}, f32[2,1,32,128]{3,2,1,0:T(8,128)S(1)}, u32[]{:S(2)}, u32[]{:S(2)}) collective-permute-start(f32[2,1,32,128]{3,2,1,0:T(8,128)S(1)} %get-tuple-element.22), channel_id=1, source_target_pairs={{0,16},{16,32},{32,48},{48,64},{64,80},{80,96},{96,112},{112,0},{1... | collective-permute-start | bytes 98312 | tf_op jit(solution)/shard_map/ppermute | solution.py:52
  61.4 8.5 %collective-permute-start.9 = (f32[2,1,32,128]{3,2,1,0:T(8,128)S(1)}, f32[2,1,32,128]{3,2,1,0:T(8,128)S(1)}, u32[]{:S(2)}, u32[]{:S(2)}) collective-permute-start(f32[2,1,32,128]{3,2,1,0:T(8,128)S(1)} %get-tuple-element.23), channel_id=1, source_target_pairs={{16,0},{32,16},{48,32},{64,48},{80,64},{96,80},{112,96},{0,112},{1... | collective-permute-start | bytes 98312 | tf_op jit(solution)/shard_map/ppermute | solution.py:53
  64.4 7.7 %collective-permute-start.10 = (f32[2,64,1,128]{3,2,1,0:T(1,128)S(1)}, f32[2,64,1,128]{3,2,1,0:T(1,128)S(1)}, u32[]{:S(2)}, u32[]{:S(2)}) collective-permute-start(f32[2,64,1,128]{3,2,1,0:T(1,128)S(1)} %get-tuple-element.20), channel_id=1, source_target_pairs={{0,1},{1,2},{2,3},{3,4},{4,5},{5,6},{6,7},{7,8},{8,9},{9,10},{10,1... | collective-permute-start | bytes 196616 | tf_op jit(solution)/shard_map/ppermute | solution.py:52
  64.5 7.6 %collective-permute-start.11 = (f32[2,64,1,128]{3,2,1,0:T(1,128)S(1)}, f32[2,64,1,128]{3,2,1,0:T(1,128)S(1)}, u32[]{:S(2)}, u32[]{:S(2)}) collective-permute-start(f32[2,64,1,128]{3,2,1,0:T(1,128)S(1)} %get-tuple-element.21), channel_id=1, source_target_pairs={{1,0},{2,1},{3,2},{4,3},{5,4},{6,5},{7,6},{8,7},{9,8},{10,9},{11,1... | collective-permute-start | bytes 196616 | tf_op jit(solution)/shard_map/ppermute | solution.py:53
  75.2 8.6 %collective-permute-start.12 = (f32[2,1,32,128]{3,2,1,0:T(8,128)S(1)}, f32[2,1,32,128]{3,2,1,0:T(8,128)S(1)}, u32[]{:S(2)}, u32[]{:S(2)}) collective-permute-start(f32[2,1,32,128]{3,2,1,0:T(8,128)S(1)} %get-tuple-element.18), channel_id=1, source_target_pairs={{0,16},{16,32},{32,48},{48,64},{64,80},{80,96},{96,112},{112,0},{1... | collective-permute-start | bytes 98312 | tf_op jit(solution)/shard_map/ppermute | solution.py:52
  75.2 8.5 %collective-permute-start.13 = (f32[2,1,32,128]{3,2,1,0:T(8,128)S(1)}, f32[2,1,32,128]{3,2,1,0:T(8,128)S(1)}, u32[]{:S(2)}, u32[]{:S(2)}) collective-permute-start(f32[2,1,32,128]{3,2,1,0:T(8,128)S(1)} %get-tuple-element.19), channel_id=1, source_target_pairs={{16,0},{32,16},{48,32},{64,48},{80,64},{96,80},{112,96},{0,112},{1... | collective-permute-start | bytes 98312 | tf_op jit(solution)/shard_map/ppermute | solution.py:53
  78.3 7.7 %collective-permute-start.14 = (f32[2,64,1,128]{3,2,1,0:T(1,128)S(1)}, f32[2,64,1,128]{3,2,1,0:T(1,128)S(1)}, u32[]{:S(2)}, u32[]{:S(2)}) collective-permute-start(f32[2,64,1,128]{3,2,1,0:T(1,128)S(1)} %get-tuple-element.16), channel_id=1, source_target_pairs={{0,1},{1,2},{2,3},{3,4},{4,5},{5,6},{6,7},{7,8},{8,9},{9,10},{10,1... | collective-permute-start | bytes 196616 | tf_op jit(solution)/shard_map/ppermute | solution.py:52
  78.4 7.6 %collective-permute-start.15 = (f32[2,64,1,128]{3,2,1,0:T(1,128)S(1)}, f32[2,64,1,128]{3,2,1,0:T(1,128)S(1)}, u32[]{:S(2)}, u32[]{:S(2)}) collective-permute-start(f32[2,64,1,128]{3,2,1,0:T(1,128)S(1)} %get-tuple-element.17), channel_id=1, source_target_pairs={{1,0},{2,1},{3,2},{4,3},{5,4},{6,5},{7,6},{8,7},{9,8},{10,9},{11,1... | collective-permute-start | bytes 196616 | tf_op jit(solution)/shard_map/ppermute | solution.py:53
where the time goes:
time: 95.7 us; the launch traced here: 95.2 us
  starting transfers between devices  41.4 us (43%)
  other arithmetic  17.4 us (18%)
  matrix products  13.9 us (15%)
  Pallas kernels  9.51 us (10%)
  waiting for transfers between devices  8.46 us (9%)
  local copies, waits for them, and re-layouts  3.43 us (4%)
  between operations  1.06 us (1%)
    ppermute x8, starting transfers between devices, with_halo(): lax.ppermute(first, axis, [(b, a) for a, b in up])  30.4 us
    dot_general x3, matrix products, select_rows(): jnp.dot(matrix, flat, precision=lax.Precision.HIGHEST, preferred_element_...  9.75 us
    pallas_call x1, Pallas kernels, physics(): pl.pallas_call(physics_kernel, out_shape=(jax.ShapeDtypeStruct((1024, 128...  9.51 us
    ppermute x8, waiting for transfers between devices, with_halo(): lax.ppermute(last, axis, up)  8.44 us
    all_to_all x1, starting transfers between devices, exchange_both(): parts = lax.all_to_all(parts, axis, split_axis=0, concat_axis=0, tiled=True)  7.67 us
    dot_general x1, matrix products, select_back(): lax.dot_general(matrix, value, (((0,), (0,)), ((), ())), precision=lax.Pr...  4.18 us
    add x3, other arithmetic, body(): start + advect_step * weight * tendency(advance(section), along_x, along_...  3.84 us
    mul x4, other arithmetic, tendency(): flux_y = along_y * (0.5 * (middle_x[:, :, :-1] + middle_x[:, :, 1:]))  3.8 us
  transfers between devices with their start and end apart: 17, of which 3 were waited for; matrix products, arithmetic and copies ran while one was open for 29% of the time, Pallas kernels for 10%

commit v1 on v0

--- a/solution.py
+++ b/solution.py
@@ -1,3 +1,5 @@
+import functools
+
 import jax
 import jax.numpy as jnp
 from jax import lax
@@ -5,9 +7,10 @@
 from jax.experimental.pallas import tpu as pltpu
 from jax.sharding import PartitionSpec as P
 
+MESH = pl.DeviceIdType.MESH
+f32 = jnp.float32
 SUBSTEPS = 6
-BLK_DEV = 512
-
+WX, WY = 66, 48
 
 clausius = 0.07
 growth = 200.0 / 3.0
@@ -17,48 +20,6 @@
 collect = 1e-07
 time_step = 2.0
 advect_step = 0.6
-
-
-def cut_along(array, dim, size):
-    before, after = (array.shape[:dim], array.shape[dim + 1 :])
-    return jnp.moveaxis(array.reshape(*before, size, -1, *after), dim, 0)
-
-
-def laid_out(parts, dim):
-    lengths = list(parts.shape[1:])
-    lengths[dim] *= parts.shape[0]
-    return jnp.moveaxis(parts, 0, dim).reshape(lengths)
-
-
-def exchange_both(array, axis, axes, splits, concats):
-    sizes = [lax.axis_size(a) for a in axes]
-    parts = cut_along(array, splits[0], sizes[0])
-    parts = jnp.moveaxis(cut_along(parts, splits[1] + 1, sizes[1]), 0, 1)
-    inside = parts.shape[2:]
-    parts = parts.reshape(-1, *inside)
-    parts = lax.all_to_all(parts, axis, split_axis=0, concat_axis=0, tiled=True)
-    parts = laid_out(parts.reshape(*sizes, *inside), concats[0] + 1)
-    return laid_out(parts, concats[1])
-
-
-def with_halo(array, sides, width):
-    edges = {}
-    for axis, dim in sides:
-        size, length = (lax.axis_size(axis), array.shape[dim])
-        up = [(i, (i + 1) % size) for i in range(size)]
-        last = lax.slice_in_dim(array, length - width, length, axis=dim)
-        first = lax.slice_in_dim(array, 0, width, axis=dim)
-        edges[dim] = (
-            lax.ppermute(last, axis, up),
-            lax.ppermute(first, axis, [(b, a) for a, b in up]),
-        )
-    done = []
-    for _, dim in sides:
-        low, high = edges[dim]
-        around = [(width, width) if d in done else (0, 0) for d in range(array.ndim)]
-        array = jnp.concatenate([jnp.pad(low, around), array, jnp.pad(high, around)], axis=dim)
-        done.append(dim)
-    return array
 
 
 def batcher(n):
@@ -184,7 +145,7 @@
                     row(xb_to, b + o)[...] = y
         loop(trips, body)
 
-def physics_kernel(rad_ref, flo_ref, mul_ref, cnt_ref, ct_ref, cv_ref, ro_ref, mo_ref, heat_ref, R, S, C, F, M, marks):
+def physics_kernel(rad_ref, flo_ref, mul_ref, cnt_ref, ct_ref, cv_ref, move_ref, send_ref, heat_ref, R, S, C, F, M, marks, X):
     def enter(g, c):
         at = pl.ds(pl.multiple_of(g * 128, 128), 128)
         to = pl.ds(g, 128, stride=8)
@@ -233,8 +194,8 @@
         weight = after
         wet = wet - condense * condensed
         temp = temp + latent * condense * condensed
-    heat_ref[0] = temp - ct_ref[...]
-    heat_ref[1] = wet - cv_ref[...]
+    heat_ref[0:8, :] = temp - ct_ref[...]
+    heat_ref[8:16, :] = wet - cv_ref[...]
 
     def radii(t, c):
         for u in range(U):
@@ -280,39 +241,287 @@
     def leave(g, c):
         at = pl.ds(pl.multiple_of(g * 128, 128), 128)
         frm = pl.ds(g, 128, stride=8)
-        ro_ref[at, :] = S[frm, :].T
-        mo_ref[at, :] = C[frm, :].T
+        for q, ref in enumerate((S, C)):
+            for k, part in enumerate(split3(ref[frm, :].T)):
+                X[at, k * 256 + q * 128:k * 256 + q * 128 + 128] = part
         return c
     lax.fori_loop(0, 8, leave, 0)
-
-def physics(radius, floor_radius, mult, counts, cell_temp, cell_vapor):
-    f32 = jnp.float32
+    moves_to = move_ref[...]
+
+    def place(n, c):
+        at = pl.multiple_of(n * 128, 128)
+        ids = lax.broadcasted_iota(jnp.int32, (128, 1024), 0) + at
+        hot = jnp.where(ids == moves_to, 1.0, 0.0).astype(jnp.bfloat16)
+        d = jnp.dot(hot, X[...], preferred_element_type=f32)
+        send_ref[pl.ds(at, 128), :] = d[:, 0:256] + (d[:, 256:512] + d[:, 512:768])
+        return c
+    lax.fori_loop(0, 8, place, 0)
+
+
+def physics(radius, floor_radius, mult, counts, cell_temp, cell_vapor, move_list):
     return pl.pallas_call(
         physics_kernel,
-        out_shape=(jax.ShapeDtypeStruct((1024, 128), f32), jax.ShapeDtypeStruct((1024, 128), f32), jax.ShapeDtypeStruct((2, 8, 128), f32)),
-        in_specs=[pl.BlockSpec(memory_space=pltpu.VMEM)] * 6,
-        out_specs=[pl.BlockSpec(memory_space=pltpu.VMEM)] * 3,
-        scratch_shapes=[pltpu.VMEM((1024, 128), f32)] * 5 + [pltpu.VMEM((N_CE * 8, 128), f32)],
+        out_shape=(jax.ShapeDtypeStruct((1024, 256), f32), jax.ShapeDtypeStruct((16, 128), f32)),
+        in_specs=[pl.BlockSpec(memory_space=pltpu.VMEM)] * 7,
+        out_specs=[pl.BlockSpec(memory_space=pltpu.VMEM)] * 2,
+        scratch_shapes=[pltpu.VMEM((1024, 128), f32)] * 5 + [pltpu.VMEM((N_CE * 8, 128), f32), pltpu.VMEM((1024, 768), jnp.bfloat16)],
         compiler_params=pltpu.CompilerParams(vmem_limit_bytes=40 * 2**20),
-        cost_estimate=pl.CostEstimate(flops=30_000_000, bytes_accessed=3_000_000, transcendentals=1_000_000),
+        cost_estimate=pl.CostEstimate(flops=1_700_000_000, bytes_accessed=3_000_000, transcendentals=1_000_000),
         name="physics",
-    )(radius, floor_radius, mult, counts, cell_temp, cell_vapor)
-
-
-def tendency(padded, along_x, along_y, along_z):
-    middle_y = padded[:, :, 1:-1]
-    flux_x = along_x * (0.5 * (middle_y[:, :-1] + middle_y[:, 1:]))
-    middle_x = padded[:, 1:-1]
-    flux_y = along_y * (0.5 * (middle_x[:, :, :-1] + middle_x[:, :, 1:]))
-    core = padded[:, 1:-1, 1:-1]
-    flux_z = along_z * (0.5 * (core[..., :-1] + core[..., 1:]))
-    edge = jnp.zeros(core.shape[:-1] + (1,), core.dtype)
-    flux_z = jnp.concatenate([edge, flux_z, edge], axis=-1)
-    return (
-        -(flux_x[:, 1:] - flux_x[:, :-1])
-        - (flux_y[:, :, 1:] - flux_y[:, :, :-1])
-        - (flux_z[..., 1:] - flux_z[..., :-1])
-    )
+    )(radius, floor_radius, mult, counts, cell_temp, cell_vapor, move_list)
+
+
+def mod(a, n):
+    return lax.rem(a + n, n)
+
+
+def split2(x):
+    hi = x.astype(jnp.bfloat16)
+    lo = (x - hi.astype(f32)).astype(jnp.bfloat16)
+    return hi, lo
+
+
+def comm_kernel(nx, ny, send_ref, t_ref, v_ref, u_ref, vv_ref, w_ref, cell_ref, zed_ref, heat_ref,
+                to_ref, vo_ref, recv_ref,
+                E, AX, AL, AH, AZ, UE, VE, yout, yin, vout, vin, W,
+                a2a_send, a2a_recv, xs, xr, ys, yr, ws, wr):
+    ix, iy = lax.axis_index("gx"), lax.axis_index("gy")
+    me = ix * ny + iy
+    count = nx * ny
+    right, left = (mod(ix + 1, nx), iy), (mod(ix - 1, nx), iy)
+    upper, lower = (ix, mod(iy + 1, ny)), (ix, mod(iy - 1, ny))
+
+    barrier = pltpu.get_barrier_semaphore()
+
+    def greet(i, c):
+        p = mod(me + i, count)
+        pl.semaphore_signal(barrier, inc=1, device_id=(p // ny, lax.rem(p, ny)), device_id_type=MESH)
+        return c
+    lax.fori_loop(1, count, greet, 0)
+
+    vout[0] = vv_ref[pl.ds(31, 64, stride=32), :]
+    vout[1] = vv_ref[pl.ds(0, 64, stride=32), :]
+    pl.semaphore_wait(barrier, count - 1)
+
+    def remote(src, dst, s, r, to):
+        return pltpu.make_async_remote_copy(src_ref=src, dst_ref=dst, send_sem=s, recv_sem=r, device_id=to, device_id_type=MESH)
+
+    winds = [
+        remote(u_ref.at[pl.ds(63 * 32, 32), :], UE.at[0], ws.at[0], wr.at[0], right),
+        remote(u_ref.at[pl.ds(0, 32), :], UE.at[1], ws.at[1], wr.at[1], left),
+        remote(vout.at[0], vin.at[0], ws.at[2], wr.at[2], upper),
+        remote(vout.at[1], vin.at[1], ws.at[3], wr.at[3], lower),
+    ]
+    for c in winds:
+        c.start()
+
+    def chunk(i):
+        p = mod(me + i, count)
+        return remote(
+            send_ref.at[pl.ds(pl.multiple_of(p * 8, 8), 8), :],
+            recv_ref.at[pl.ds(pl.multiple_of(me * 8, 8), 8), :],
+            a2a_send, a2a_recv, (p // ny, lax.rem(p, ny)))
+
+    def send_some(lo, hi):
+        def body(i, c):
+            chunk(i).start()
+            return c
+        lax.fori_loop(lo, hi, body, 0)
+
+    send_some(1, count // 3)
+    mine = pl.ds(pl.multiple_of(me * 8, 8), 8)
+    recv_ref[mine, :] = send_ref[mine, :]
+
+    zed = lax.rem(zed_ref[...], 128).astype(f32).T.astype(jnp.int32)
+    heat = heat_ref[...].T
+    lanes = lax.broadcasted_iota(jnp.int32, (128, 128), 1)
+    for g in range(8):
+        level = lanes == zed[:, g:g + 1]
+        at = pl.ds(g * 128, 128)
+        for q in range(2):
+            h = jnp.where(level, heat[:, q * 8 + g:q * 8 + g + 1], 0.0)
+            hi, lo = split2(h)
+            W[at, q * 128:q * 128 + 128] = hi
+            W[at, 256 + q * 128:256 + q * 128 + 128] = lo
+    cells = lax.shift_right_logical(cell_ref[...], 7)
+
+    def scatter(k, c):
+        at = pl.multiple_of(k * 128, 128)
+        ids = lax.broadcasted_iota(jnp.int32, (128, 1024), 0) + at
+        hot = jnp.where(ids == cells, 1.0, 0.0).astype(jnp.bfloat16)
+        d = jnp.dot(hot, W[...], preferred_element_type=f32)
+        for q, ref in ((0, t_ref), (1, v_ref)):
+            add = d[:, q * 128:q * 128 + 128] + d[:, 256 + q * 128:256 + q * 128 + 128]
+            new = ref[pl.ds(at, 128), :] + add
+            for j in range(4):
+                E[q, pl.ds(pl.multiple_of((k * 4 + j + 1) * WY + 8, 8), 32), :] = new[j * 32:j * 32 + 32]
+        return c
+    lax.fori_loop(0, 16, scatter, 0)
+
+    def plane(x):
+        return x * WY + 8
+
+    def exchange(s):
+        moves = []
+        for q in range(2):
+            e = E.at[2 * s + q]
+            moves.append(remote(e.at[pl.ds(plane(64), 32), :], e.at[pl.ds(plane(0), 32), :], xs.at[4 * s + 2 * q], xr.at[4 * s + 2 * q], right))
+            moves.append(remote(e.at[pl.ds(plane(1), 32), :], e.at[pl.ds(plane(65), 32), :], xs.at[4 * s + 2 * q + 1], xr.at[4 * s + 2 * q + 1], left))
+            yout[2 * s, pl.ds(64 * q, 64), :] = E[2 * s + q, pl.ds(plane(1) + 31, 64, stride=WY), :]
+            yout[2 * s + 1, pl.ds(64 * q, 64), :] = E[2 * s + q, pl.ds(plane(1), 64, stride=WY), :]
+        moves.append(remote(yout.at[2 * s], yin.at[2 * s], ys.at[2 * s], yr.at[2 * s], upper))
+        moves.append(remote(yout.at[2 * s + 1], yin.at[2 * s + 1], ys.at[2 * s + 1], yr.at[2 * s + 1], lower))
+        for c in moves:
+            c.start()
+        return moves
+
+    def arrive(s, moves):
+        for c in moves:
+            c.wait_recv()
+        for q in range(2):
+            E[2 * s + q, pl.ds(plane(1) - 1, 64, stride=WY), :] = yin[2 * s, pl.ds(64 * q, 64), :]
+            E[2 * s + q, pl.ds(plane(1) + 32, 64, stride=WY), :] = yin[2 * s + 1, pl.ds(64 * q, 64), :]
+
+    moves = exchange(0)
+    send_some(count // 3, 2 * count // 3)
+    for c in winds:
+        c.wait_recv()
+
+    AX[pl.ds(0, 32), :] = 0.25 * (UE[0] + u_ref[pl.ds(0, 32), :])
+    AX[pl.ds(64 * 32, 32), :] = 0.25 * (u_ref[pl.ds(63 * 32, 32), :] + UE[1])
+    VE[pl.ds(7, 64, stride=WY), :] = vin[0]
+    VE[pl.ds(40, 64, stride=WY), :] = vin[1]
+    last = lax.broadcasted_iota(jnp.int32, (32, 128), 1) == 127
+
+    def enter(x, c):
+        at = pl.ds(pl.multiple_of(x * 32, 32), 32)
+        VE[pl.ds(pl.multiple_of(x * WY + 8, 8), 32), :] = vv_ref[at, :]
+        return c
+    lax.fori_loop(0, 64, enter, 0)
+
+    def faces(x, c):
+        at = pl.ds(pl.multiple_of(x * 32, 32), 32)
+        here = vv_ref[at, :]
+        AL[at, :] = 0.25 * (here + VE[pl.ds(x * WY + 7, 32), :])
+        AH[at, :] = 0.25 * (here + VE[pl.ds(x * WY + 9, 32), :])
+        w = w_ref[at, :]
+        AZ[at, :] = jnp.where(last, 0.0, 0.25 * (w + pltpu.roll(w, 127, 1)))
+        return c
+    lax.fori_loop(0, 64, faces, 0)
+
+    def face_x(x, c):
+        AX[pl.ds(pl.multiple_of(x * 32, 32), 32), :] = 0.25 * (u_ref[pl.ds(pl.multiple_of(x * 32 - 32, 32), 32), :] + u_ref[pl.ds(pl.multiple_of(x * 32, 32), 32), :])
+        return c
+    lax.fori_loop(1, 64, face_x, 0)
+
+    for s, weight in enumerate((advect_step / 3.0, advect_step / 2.0, advect_step)):
+        arrive(s, moves)
+        for q in range(2):
+            src = E.at[2 * s + q]
+            start = E.at[q]
+            def step(x, carry, q=q, src=src, start=start, s=s, weight=weight):
+                f, low = carry
+                at = pl.ds(pl.multiple_of(x * 32, 32), 32)
+                p = pl.multiple_of((x + 1) * WY + 8, 8)
+                after = src[pl.ds(pl.multiple_of(p + WY, 8), 32), :]
+                high = AX[pl.ds(pl.multiple_of(x * 32 + 32, 32), 32), :] * (f + after)
+                fy = AH[at, :] * (f + src[pl.ds(p + 1, 32), :]) - AL[at, :] * (src[pl.ds(p - 1, 32), :] + f)
+                fz = AZ[at, :] * (f + pltpu.roll(f, 127, 1))
+                out = start[pl.ds(p, 32), :] - weight * ((high - low) + fy + (fz - pltpu.roll(fz, 1, 1)))
+                if s < 2:
+                    E[2 * s + 2 + q, pl.ds(p, 32), :] = out
+                else:
+                    (to_ref, vo_ref)[q][at, :] = out
+                return after, high
+            f0 = src[pl.ds(plane(1), 32), :]
+            lax.fori_loop(0, 64, step, (f0, AX[pl.ds(0, 32), :] * (src[pl.ds(plane(0), 32), :] + f0)))
+        for c in moves:
+            c.wait_send()
+        if s < 2:
+            moves = exchange(s + 1)
+        if s == 0:
+            send_some(2 * count // 3, count)
+    for c in winds:
+        c.wait_send()
+    whole = remote(recv_ref.at[pl.ds(8, 8 * (count - 1)), :], recv_ref.at[pl.ds(8, 8 * (count - 1)), :], a2a_send, a2a_recv, right)
+    whole.wait_send()
+    whole.wait_recv()
+
+
+def comm(mesh_shape, send, t, v, u, vv, w, cells, zed, heat):
+    nx, ny = mesh_shape
+    VM = pl.BlockSpec(memory_space=pltpu.VMEM)
+    bf16 = jnp.bfloat16
+    DMA = pltpu.SemaphoreType.DMA
+    return pl.pallas_call(
+        functools.partial(comm_kernel, nx, ny),
+        out_shape=(jax.ShapeDtypeStruct((2048, 128), f32), jax.ShapeDtypeStruct((2048, 128), f32), jax.ShapeDtypeStruct((1024, 256), f32)),
+        in_specs=[VM] * 9,
+        out_specs=[VM] * 3,
+        scratch_shapes=[
+            pltpu.VMEM((6, WX * WY, 128), f32),
+            pltpu.VMEM((65 * 32, 128), f32), pltpu.VMEM((2048, 128), f32), pltpu.VMEM((2048, 128), f32), pltpu.VMEM((2048, 128), f32),
+            pltpu.VMEM((2, 32, 128), f32), pltpu.VMEM((64 * WY, 128), f32),
+            pltpu.VMEM((6, 128, 128), f32), pltpu.VMEM((6, 128, 128), f32),
+            pltpu.VMEM((2, 64, 128), f32), pltpu.VMEM((2, 64, 128), f32),
+            pltpu.VMEM((1024, 512), bf16),
+            DMA, DMA, DMA((12,)), DMA((12,)), DMA((6,)), DMA((6,)), DMA((4,)), DMA((4,)),
+        ],
+        compiler_params=pltpu.CompilerParams(vmem_limit_bytes=56 * 2**20, collective_id=0, has_side_effects=True),
+        cost_estimate=pl.CostEstimate(flops=3_000_000_000, bytes_accessed=8_000_000, transcendentals=0),
+        name="exchange",
+    )(send, t, v, u, vv, w, cells, zed, heat)
+
+
+def triangle(n):
+    return lax.broadcasted_iota(jnp.int32, (n, n), 0) < lax.broadcasted_iota(jnp.int32, (n, n), 1)
+
+
+def split3(x):
+    hi = x.astype(jnp.bfloat16)
+    rest = x - hi.astype(f32)
+    mid = rest.astype(jnp.bfloat16)
+    return hi, mid, (rest - mid.astype(f32)).astype(jnp.bfloat16)
+
+
+def compact_kernel(recv_ref, ro_ref, mo_ref, X):
+    rows = []
+    for g in range(8):
+        rows.append(recv_ref[pl.ds(g * 128, 128), 128:256].T[0:1])
+    first = jnp.concatenate(rows, axis=0)
+    taken = jnp.where(first > 0.0, 1.0, 0.0)
+    within = jnp.dot(taken.astype(jnp.bfloat16), jnp.where(triangle(128), 1.0, 0.0).astype(jnp.bfloat16), preferred_element_type=f32)
+    total = jnp.sum(taken, axis=1, keepdims=True)
+    pos = []
+    before = jnp.zeros((1, 1), f32)
+    for g in range(8):
+        pos.append(jnp.where(first[g:g + 1] > 0.0, within[g:g + 1] + before, -1.0))
+        before = before + total[g:g + 1]
+    pos = jnp.concatenate(pos, axis=1).astype(jnp.int32)
+    for g in range(8):
+        at = pl.ds(g * 128, 128)
+        for k, part in enumerate(split3(recv_ref[at, :])):
+            X[at, k * 256:k * 256 + 256] = part
+    for n in range(4):
+        ids = lax.broadcasted_iota(jnp.int32, (128, 1024), 0) + n * 128
+        hot = jnp.where(ids == pos, 1.0, 0.0).astype(jnp.bfloat16)
+        d = jnp.dot(hot, X[...], preferred_element_type=f32)
+        d = d[:, 0:256] + (d[:, 256:512] + d[:, 512:768])
+        ro_ref[pl.ds(n * 128, 128), :] = d[:, 0:128]
+        mo_ref[pl.ds(n * 128, 128), :] = d[:, 128:256]
+
+
+def compacted(recv):
+    VM = pl.BlockSpec(memory_space=pltpu.VMEM)
+    return pl.pallas_call(
+        compact_kernel,
+        out_shape=(jax.ShapeDtypeStruct((512, 128), f32), jax.ShapeDtypeStruct((512, 128), f32)),
+        in_specs=[VM], out_specs=[VM, VM],
+        scratch_shapes=[pltpu.VMEM((1024, 768), jnp.bfloat16)],
+        compiler_params=pltpu.CompilerParams(vmem_limit_bytes=16 * 2**20),
+        cost_estimate=pl.CostEstimate(flops=800_000_000, bytes_accessed=2_000_000, transcendentals=0),
+        name="compact",
+    )(recv)
 
 
 def selector(index, count):
@@ -327,37 +536,8 @@
     return picked.reshape((matrix.shape[0],) + value.shape[1:])
 
 
-def select_back(matrix, value):
-    picked = lax.dot_general(
-        matrix,
-        value,
-        (((0,), (0,)), ((), ())),
-        precision=lax.Precision.HIGHEST,
-        preferred_element_type=jnp.float32,
-    )
-    return picked
-
-
-def single(value, cap):
-    lead = (lax.axis_size("gx"), lax.axis_size("gy"), cap)
-    moved = exchange_both(
-        value.reshape(lead + value.shape[1:]), ("gx", "gy"), ("gx", "gy"), (0, 1), (0, 1)
-    )
-    return moved.reshape(value.shape)
-
-
-def compact(taken):
-    position = jnp.cumsum(taken.astype(jnp.int32)) - 1
-    target = jnp.where(taken, position, BLK_DEV)
-    return selector(target, BLK_DEV)
-
-
-def advance(state):
-    padded = with_halo(state, (("gx", 1), ("gy", 2)), 1)
-    return padded
-
-
 def body(
+    shape,
     tprime,
     vapor,
     wind_u,
@@ -370,55 +550,35 @@
     cell_index,
     move_list,
 ):
-    devices = lax.axis_size("gx") * lax.axis_size("gy")
     home = radius.shape[0]
-    drops = radius.shape[1]
-    cap = (home + devices - 1) // devices
-    slots = devices * cap
     columns = tprime.shape[0] * tprime.shape[1]
     levels = tprime.shape[2]
-    live = move_list >= 0
-    target = jnp.where(live, move_list, slots)
-    placing = selector(target, slots)
+    flat = [a.reshape(columns, levels) for a in (tprime, vapor, wind_u, wind_v, wind_w)]
     column_pick = selector(cell_index // levels, columns).T
     level_pick = selector(cell_index % levels, levels).T
-    fields = jnp.concatenate(
-        [tprime.reshape(columns, levels), vapor.reshape(columns, levels)], axis=1
-    )
-    at_column = select_rows(column_pick, fields)
+    at_column = select_rows(column_pick, jnp.concatenate(flat[:2], axis=1))
     cell_temp = jnp.sum(at_column[:, :levels] * level_pick, axis=1)
     cell_vapor = jnp.sum(at_column[:, levels:] * level_pick, axis=1)
     square = (8, home // 8)
-    radius_new, mult_new, heat = physics(
+    send, heat = physics(
         radius,
         min_radius,
         multiplicity,
         drop_counts.reshape(square),
         cell_temp.reshape(square),
         cell_vapor.reshape(square),
+        move_list.reshape(1, home),
     )
-    bulk = single(select_rows(placing, jnp.concatenate([radius_new, mult_new], axis=1)), cap)
-    gather_rows = compact(bulk[:, drops] > 0.0)
-    picked = select_rows(gather_rows, bulk)
-    radius_out = picked[:, :drops]
-    multiplicity_out = picked[:, drops:]
-    heat_t = heat[0].reshape(home)
-    heat_v = heat[1].reshape(home)
-    weighted = jnp.concatenate([level_pick * heat_t[:, None], level_pick * heat_v[:, None]], axis=1)
-    added = select_back(column_pick, weighted)
-    heated_t = (fields[:, :levels] + added[:, :levels]).reshape(tprime.shape)
-    heated_v = (fields[:, levels:] + added[:, levels:]).reshape(vapor.shape)
-    winds = with_halo(jnp.stack([wind_u, wind_v]), (("gx", 1), ("gy", 2)), 1)
-    along_x = 0.5 * (winds[0, :-1, 1:-1] + winds[0, 1:, 1:-1])
-    along_y = 0.5 * (winds[1, 1:-1, :-1] + winds[1, 1:-1, 1:])
-    along_z = 0.5 * (wind_w[..., :-1] + wind_w[..., 1:])
-    start = jnp.stack([heated_t, heated_v])
-    section = start
-    for weight in (1.0 / 3.0, 0.5, 1.0):
-        section = start + advect_step * weight * tendency(
-            advance(section), along_x, along_y, along_z
-        )
-    return (section[0], section[1], radius_out, multiplicity_out)
+    temperature, humidity, recv = comm(
+        shape, send, *flat, cell_index.reshape(1, home), cell_index.reshape(square), heat
+    )
+    radius_out, multiplicity_out = compacted(recv)
+    return (
+        temperature.reshape(tprime.shape),
+        humidity.reshape(vapor.shape),
+        radius_out,
+        multiplicity_out,
+    )
 
 
 def solution(mesh):
@@ -436,7 +596,7 @@
         P(("gx", "gy")),
     )
     return jax.shard_map(
-        body,
+        functools.partial(body, (mesh.shape["gx"], mesh.shape["gy"])),
         mesh=mesh,
         in_specs=placed,
         out_specs=(

time: 95.7 us -> 124 us (1.30)
  Pallas kernels: 9.51 us -> 110 us
  starting transfers between devices: 41.4 us -> 0 us
  other arithmetic: 17.4 us -> 0.81 us
  waiting for transfers between devices: 8.46 us -> 0 us
  matrix products: 13.9 us -> 5.79 us
  local copies, waits for them, and re-layouts: 3.43 us -> 6.41 us
    pallas_call x1 -> x3, Pallas kernels: 9.51 us -> 110 us  [the longest x1 95.7 us: comm(): pl.pallas_call(functools.partial(comm_kernel, nx, ny), out_shape=(jax.Sha...]
    ppermute x16 -> x0, starting transfers between devices: 33.7 us -> none  [the longest x8 30.4 us: with_halo(): lax.ppermute(first, axis, [(b, a) for a, b in up])]
    mul x13 -> x0, other arithmetic: 8.96 us -> none  [the longest x4 3.8 us: tendency(): flux_y = along_y * (0.5 * (middle_x[:, :, :-1] + middle_x[:, :, 1:]))]
    ppermute x16 -> x0, waiting for transfers between devices: 8.46 us -> none  [the longest x8 8.44 us: with_halo(): lax.ppermute(last, axis, up)]
    all_to_all x1 -> x0, starting transfers between devices: 7.67 us -> none  [exchange_both(): parts = lax.all_to_all(parts, axis, split_axis=0, concat_axis=0, tiled=True)]
    unnamed x24 -> x22, local copies, waits for them, and re-layouts: 0.73 us -> 6.41 us
    dot_general x1 -> x0, matrix products: 4.18 us -> none  [select_back(): lax.dot_general(matrix, value, (((0,), (0,)), ((), ())), precision=lax.Pr...]
    add x4 -> x0, other arithmetic: 4.17 us -> none  [the longest x3 3.84 us: body(): start + advect_step * weight * tendency(advance(section), along_x, along_...]
  transfers between devices with their start and end apart: 17 -> 0, of which waited for: 3 -> 0; matrix products, arithmetic and copies ran while one was open for 29% -> 0% of each run, Pallas kernels for 10% -> 0%
where the time goes in v1:
time: 124 us
  Pallas kernels  110 us (89%)
  local copies, waits for them, and re-layouts  6.41 us (5%)
  matrix products  5.79 us (5%)
    pallas_call x1, Pallas kernels, comm(): pl.pallas_call(functools.partial(comm_kernel, nx, ny), out_shape=(jax.Sha...  95.7 us
    pallas_call x1, Pallas kernels, physics(): pl.pallas_call(physics_kernel, out_shape=(jax.ShapeDtypeStruct((1024, 256...  12.4 us
    unnamed x22, local copies, waits for them, and re-layouts  6.41 us
    dot_general x1, matrix products, select_rows(): jnp.dot(matrix, flat, precision=lax.Precision.HIGHEST, preferred_element_...  5.79 us

profile of v1, /device:TPU:0, one launch (start us, length us, event | category | flops | bytes accessed | tf_op | source)
XLA Modules:
  0.0 124.0 jit_solution(7142412032807912792)
XLA Ops:
  0.6 0.7 add_select_fusion.1
  1.3 0.0 copy-start.2
  1.3 5.8 %fusion = f32[1024,256]{0,1:T(8,128)S(1)} fusion(s32[1024]{0:T(1024)S(1)} %get-tuple-element.21, f32[2048,128]{1,0:T(8,128)} %bitcast.21, f32[2048,128]{1,0:T(8,128)} %bitcast.23), kind=kOutput, calls=%fused_computation.1 | convolution fusion | flops 6445072384 | bytes 3149824 | tf_op jit(solution)/shard_map/dot_general | solution.py:533
  7.1 0.0 copy-start
  7.1 0.0 copy-start.1
  7.2 0.0 copy-start.3
  7.2 0.0 copy-start.4
  7.2 0.1 fusion.5
  7.3 0.0 copy-done.2
  7.3 0.9 copy-done
  8.2 0.2 copy-done.1
  8.3 0.0 copy-done.3
  8.3 0.0 copy-done.4
  8.3 12.4 %physics.1 = (f32[1024,256]{1,0:T(8,128)S(1)}, f32[16,128]{1,0:T(8,128)S(1)}) custom-call(f32[1024,128]{1,0:T(8,128)S(1)} %copy-done, f32[1024,128]{1,0:T(8,128)S(1)} %copy-done.1, f32[1024,128]{1,0:T(8,128)S(1)} %copy-done.2, s32[8,128]{1,0:T(8,128)S(1)} %bitcast.15, f32[8,128]{1,0:T(8,128)S(1)} %bitcast.14, f32[8,128]{1,0:T(8,128)S(1)} %bitcast.13, ...), custom_call_target="tpu_custom_call" | custom-call | flops 1700000000 | bytes 3000000 | tf_op jit(solution)/shard_map/physics/pallas_call | solution.py:262
  20.8 0.0 copy-start.6
  20.8 1.0 copy-done.6
  21.8 0.0 copy-start.7
  21.8 0.6 copy-done.7
  22.4 95.7 %exchange.1 = (f32[2048,128]{1,0:T(8,128)}, f32[2048,128]{1,0:T(8,128)}, f32[1024,256]{1,0:T(8,128)}) custom-call(f32[1024,256]{1,0:T(8,128)} %copy-done.6, f32[2048,128]{1,0:T(8,128)} %bitcast.24, f32[2048,128]{1,0:T(8,128)} %bitcast.22, f32[2048,128]{1,0:T(8,128)} %bitcast.25, f32[2048,128]{1,0:T(8,128)} %bitcast.26, f32[2048,128]{1,0:T(8,128)} %bitcast.27, ...), custom_call_target="tpu_custom_call" | custom-call | flops 3000000000 | bytes 8000000 | tf_op jit(solution)/shard_map/exchange/pallas_call | solution.py:456
  118.1 0.0 copy-start.5
  118.1 1.2 copy-done.5
  119.3 0.0 copy-start.9
  119.3 2.1 %compact.1 = (f32[512,128]{1,0:T(8,128)}, f32[512,128]{1,0:T(8,128)}) custom-call(f32[1024,256]{1,0:T(8,128)S(1)} %copy-done.5), custom_call_target="tpu_custom_call" | custom-call | flops 800000000 | bytes 2000000 | tf_op jit(solution)/shard_map/compact/pallas_call | solution.py:516
  121.4 0.0 copy-done.9
  121.4 0.0 copy-start.8
  121.4 1.0 copy.17
  122.4 0.6 copy-done.8
  123.0 1.0 copy.18
Async XLA Ops:
  1.3 6.0 %copy-start.2 = (f32[1024,128]{1,0:T(8,128)S(1)}, f32[1024,128]{1,0:T(8,128)}, u32[]{:S(2)}) copy-start(f32[1024,128]{1,0:T(8,128)} %mul_ref.1) | copy-start | bytes 1572868
  7.1 1.0 copy-start
  7.1 1.2 copy-start.1
  7.2 1.2 copy-start.3
  7.2 1.2 copy-start.4
  20.8 1.0 copy-start.6
  21.8 0.6 copy-start.7
  118.1 1.2 copy-start.5
  119.3 2.1 %copy-start.9 = (f32[2048,128]{1,0:T(8,128)S(1)}, f32[2048,128]{1,0:T(8,128)}, u32[]{:S(2)}) copy-start(f32[2048,128]{1,0:T(8,128)} %get-tuple-element.13) | copy-start | bytes 3145732
  121.4 1.6 %copy-start.8 = (f32[2048,128]{1,0:T(8,128)S(1)}, f32[2048,128]{1,0:T(8,128)}, u32[]{:S(2)}) copy-start(f32[2048,128]{1,0:T(8,128)} %get-tuple-element.14) | copy-start | bytes 3145732

commit v2 on v1

--- a/solution.py
+++ b/solution.py
@@ -11,6 +11,7 @@
 f32 = jnp.float32
 SUBSTEPS = 6
 WX, WY = 66, 48
+UNROLL = 8
 
 clausius = 0.07
 growth = 200.0 / 3.0
@@ -145,7 +146,27 @@
                     row(xb_to, b + o)[...] = y
         loop(trips, body)
 
-def physics_kernel(rad_ref, flo_ref, mul_ref, cnt_ref, ct_ref, cv_ref, move_ref, send_ref, heat_ref, R, S, C, F, M, marks, X):
+def gather_cells(index, t_ref, v_ref, cell_ref, ct, cv, T, V):
+    def rows(k, c):
+        for j in range(16):
+            b = k * 16 + j
+            at = lax.shift_right_logical(index[b], 7)
+            T[pl.ds(b, 1), :] = t_ref[pl.ds(at, 1), :]
+            V[pl.ds(b, 1), :] = v_ref[pl.ds(at, 1), :]
+        return c
+    lax.fori_loop(0, 64, rows, 0)
+    level = lax.rem(cell_ref[...], 128)
+    depth = lax.broadcasted_iota(jnp.int32, (128, 128), 0)
+    for g in range(8):
+        here = depth == level[g:g + 1]
+        for staged, cell in ((T, ct), (V, cv)):
+            picked = jnp.where(here, staged[pl.ds(g * 128, 128), :].T, 0.0)
+            cell[pl.ds(g, 1), :] = jnp.sum(picked, axis=0, keepdims=True)
+
+
+def physics_kernel(index, t_ref, v_ref, rad_ref, flo_ref, mul_ref, cnt_ref, cell_ref, move_ref, send_ref, heat_ref, R, S, C, F, M, marks, X, ct_ref, cv_ref):
+    gather_cells(index, t_ref, v_ref, cell_ref, ct_ref, cv_ref, S, C)
+
     def enter(g, c):
         at = pl.ds(pl.multiple_of(g * 128, 128), 128)
         to = pl.ds(g, 128, stride=8)
@@ -258,17 +279,18 @@
     lax.fori_loop(0, 8, place, 0)
 
 
-def physics(radius, floor_radius, mult, counts, cell_temp, cell_vapor, move_list):
+def physics(index, t, v, radius, floor_radius, mult, counts, cells, move_list):
+    VM = pl.BlockSpec(memory_space=pltpu.VMEM)
     return pl.pallas_call(
         physics_kernel,
         out_shape=(jax.ShapeDtypeStruct((1024, 256), f32), jax.ShapeDtypeStruct((16, 128), f32)),
-        in_specs=[pl.BlockSpec(memory_space=pltpu.VMEM)] * 7,
-        out_specs=[pl.BlockSpec(memory_space=pltpu.VMEM)] * 2,
-        scratch_shapes=[pltpu.VMEM((1024, 128), f32)] * 5 + [pltpu.VMEM((N_CE * 8, 128), f32), pltpu.VMEM((1024, 768), jnp.bfloat16)],
-        compiler_params=pltpu.CompilerParams(vmem_limit_bytes=40 * 2**20),
+        in_specs=[pl.BlockSpec(memory_space=pltpu.SMEM)] + [VM] * 8,
+        out_specs=[VM] * 2,
+        scratch_shapes=[pltpu.VMEM((1024, 128), f32)] * 5 + [pltpu.VMEM((N_CE * 8, 128), f32), pltpu.VMEM((1024, 768), jnp.bfloat16), pltpu.VMEM((8, 128), f32), pltpu.VMEM((8, 128), f32)],
+        compiler_params=pltpu.CompilerParams(vmem_limit_bytes=20 * 2**20),
         cost_estimate=pl.CostEstimate(flops=1_700_000_000, bytes_accessed=3_000_000, transcendentals=1_000_000),
         name="physics",
-    )(radius, floor_radius, mult, counts, cell_temp, cell_vapor, move_list)
+    )(index, t, v, radius, floor_radius, mult, counts, cells, move_list)
 
 
 def mod(a, n):
@@ -283,8 +305,8 @@
 
 def comm_kernel(nx, ny, send_ref, t_ref, v_ref, u_ref, vv_ref, w_ref, cell_ref, zed_ref, heat_ref,
                 to_ref, vo_ref, recv_ref,
-                E, AX, AL, AH, AZ, UE, VE, yout, yin, vout, vin, W,
-                a2a_send, a2a_recv, xs, xr, ys, yr, ws, wr):
+                E, AX, AL, AH, AZ, AD, UE, VE, yout, yin, vout, vin, W,
+                a2a_send, a2a_recv, xs, xr, ys, yr, ws, wr, rows):
     ix, iy = lax.axis_index("gx"), lax.axis_index("gy")
     me = ix * ny + iy
     count = nx * ny
@@ -293,15 +315,16 @@
 
     barrier = pltpu.get_barrier_semaphore()
 
-    def greet(i, c):
-        p = mod(me + i, count)
-        pl.semaphore_signal(barrier, inc=1, device_id=(p // ny, lax.rem(p, ny)), device_id_type=MESH)
-        return c
-    lax.fori_loop(1, count, greet, 0)
+    for i in range(1, ny):
+        pl.semaphore_signal(barrier, inc=1, device_id=(ix, mod(iy + i, ny)), device_id_type=MESH)
+    for i in range(1, nx):
+        pl.semaphore_signal(barrier, inc=1, device_id=(mod(ix + i, nx), iy), device_id_type=MESH)
 
     vout[0] = vv_ref[pl.ds(31, 64, stride=32), :]
     vout[1] = vv_ref[pl.ds(0, 64, stride=32), :]
-    pl.semaphore_wait(barrier, count - 1)
+    pl.semaphore_wait(barrier, nx + ny - 2)
+    for i in range(1, ny):
+        pl.semaphore_signal(rows, inc=1, device_id=(ix, mod(iy + i, ny)), device_id_type=MESH)
 
     def remote(src, dst, s, r, to):
         return pltpu.make_async_remote_copy(src_ref=src, dst_ref=dst, send_sem=s, recv_sem=r, device_id=to, device_id_type=MESH)
@@ -328,6 +351,7 @@
             return c
         lax.fori_loop(lo, hi, body, 0)
 
+    pl.semaphore_wait(rows, ny - 1)
     send_some(1, count // 3)
     mine = pl.ds(pl.multiple_of(me * 8, 8), 8)
     recv_ref[mine, :] = send_ref[mine, :]
@@ -391,50 +415,59 @@
     AX[pl.ds(64 * 32, 32), :] = 0.25 * (u_ref[pl.ds(63 * 32, 32), :] + UE[1])
     VE[pl.ds(7, 64, stride=WY), :] = vin[0]
     VE[pl.ds(40, 64, stride=WY), :] = vin[1]
-    last = lax.broadcasted_iota(jnp.int32, (32, 128), 1) == 127
-
-    def enter(x, c):
-        at = pl.ds(pl.multiple_of(x * 32, 32), 32)
-        VE[pl.ds(pl.multiple_of(x * WY + 8, 8), 32), :] = vv_ref[at, :]
-        return c
-    lax.fori_loop(0, 64, enter, 0)
-
-    def faces(x, c):
-        at = pl.ds(pl.multiple_of(x * 32, 32), 32)
-        here = vv_ref[at, :]
-        AL[at, :] = 0.25 * (here + VE[pl.ds(x * WY + 7, 32), :])
-        AH[at, :] = 0.25 * (here + VE[pl.ds(x * WY + 9, 32), :])
-        w = w_ref[at, :]
-        AZ[at, :] = jnp.where(last, 0.0, 0.25 * (w + pltpu.roll(w, 127, 1)))
-        return c
-    lax.fori_loop(0, 64, faces, 0)
-
-    def face_x(x, c):
-        AX[pl.ds(pl.multiple_of(x * 32, 32), 32), :] = 0.25 * (u_ref[pl.ds(pl.multiple_of(x * 32 - 32, 32), 32), :] + u_ref[pl.ds(pl.multiple_of(x * 32, 32), 32), :])
-        return c
-    lax.fori_loop(1, 64, face_x, 0)
+    lane = lax.broadcasted_iota(jnp.int32, (32, 128), 1)
+
+    def enter(k, c):
+        for j in range(8):
+            x = k * 8 + j
+            VE[pl.ds(pl.multiple_of(x * WY + 8, 8), 32), :] = vv_ref[pl.ds(pl.multiple_of(x * 32, 32), 32), :]
+        return c
+    lax.fori_loop(0, 8, enter, 0)
+
+    def faces(k, c):
+        for j in range(4):
+            x = k * 4 + j
+            at = pl.ds(pl.multiple_of(x * 32, 32), 32)
+            here = vv_ref[at, :]
+            AL[at, :] = 0.25 * (here + VE[pl.ds(x * WY + 7, 32), :])
+            AH[at, :] = 0.25 * (here + VE[pl.ds(x * WY + 9, 32), :])
+            w = w_ref[at, :]
+            AZ[at, :] = jnp.where(lane == 127, 0.0, 0.25 * (w + pltpu.roll(w, 127, 1)))
+            AD[at, :] = jnp.where(lane == 0, 0.0, 0.25 * (w + pltpu.roll(w, 1, 1)))
+        return c
+    lax.fori_loop(0, 16, faces, 0)
+
+    def face_x(k, c):
+        for j in range(7):
+            x = k * 7 + j + 1
+            AX[pl.ds(pl.multiple_of(x * 32, 32), 32), :] = 0.25 * (u_ref[pl.ds(pl.multiple_of(x * 32 - 32, 32), 32), :] + u_ref[pl.ds(pl.multiple_of(x * 32, 32), 32), :])
+        return c
+    lax.fori_loop(0, 9, face_x, 0)
 
     for s, weight in enumerate((advect_step / 3.0, advect_step / 2.0, advect_step)):
         arrive(s, moves)
         for q in range(2):
             src = E.at[2 * s + q]
             start = E.at[q]
-            def step(x, carry, q=q, src=src, start=start, s=s, weight=weight):
+            def step(k, carry, q=q, src=src, start=start, s=s, weight=weight):
                 f, low = carry
-                at = pl.ds(pl.multiple_of(x * 32, 32), 32)
-                p = pl.multiple_of((x + 1) * WY + 8, 8)
-                after = src[pl.ds(pl.multiple_of(p + WY, 8), 32), :]
-                high = AX[pl.ds(pl.multiple_of(x * 32 + 32, 32), 32), :] * (f + after)
-                fy = AH[at, :] * (f + src[pl.ds(p + 1, 32), :]) - AL[at, :] * (src[pl.ds(p - 1, 32), :] + f)
-                fz = AZ[at, :] * (f + pltpu.roll(f, 127, 1))
-                out = start[pl.ds(p, 32), :] - weight * ((high - low) + fy + (fz - pltpu.roll(fz, 1, 1)))
-                if s < 2:
-                    E[2 * s + 2 + q, pl.ds(p, 32), :] = out
-                else:
-                    (to_ref, vo_ref)[q][at, :] = out
-                return after, high
+                for j in range(UNROLL):
+                    x = k * UNROLL + j
+                    at = pl.ds(pl.multiple_of(x * 32, 32), 32)
+                    p = pl.multiple_of((x + 1) * WY + 8, 8)
+                    after = src[pl.ds(pl.multiple_of(p + WY, 8), 32), :]
+                    high = AX[pl.ds(pl.multiple_of(x * 32 + 32, 32), 32), :] * (f + after)
+                    fy = AH[at, :] * (f + src[pl.ds(p + 1, 32), :]) - AL[at, :] * (src[pl.ds(p - 1, 32), :] + f)
+                    fz = AZ[at, :] * (f + pltpu.roll(f, 127, 1)) - AD[at, :] * (pltpu.roll(f, 1, 1) + f)
+                    out = start[pl.ds(p, 32), :] - weight * ((high - low) + fy + fz)
+                    if s < 2:
+                        E[2 * s + 2 + q, pl.ds(p, 32), :] = out
+                    else:
+                        (to_ref, vo_ref)[q][at, :] = out
+                    f, low = after, high
+                return f, low
             f0 = src[pl.ds(plane(1), 32), :]
-            lax.fori_loop(0, 64, step, (f0, AX[pl.ds(0, 32), :] * (src[pl.ds(plane(0), 32), :] + f0)))
+            lax.fori_loop(0, 64 // UNROLL, step, (f0, AX[pl.ds(0, 32), :] * (src[pl.ds(plane(0), 32), :] + f0)))
         for c in moves:
             c.wait_send()
         if s < 2:
@@ -460,14 +493,14 @@
         out_specs=[VM] * 3,
         scratch_shapes=[
             pltpu.VMEM((6, WX * WY, 128), f32),
-            pltpu.VMEM((65 * 32, 128), f32), pltpu.VMEM((2048, 128), f32), pltpu.VMEM((2048, 128), f32), pltpu.VMEM((2048, 128), f32),
+            pltpu.VMEM((65 * 32, 128), f32), pltpu.VMEM((2048, 128), f32), pltpu.VMEM((2048, 128), f32), pltpu.VMEM((2048, 128), f32), pltpu.VMEM((2048, 128), f32),
             pltpu.VMEM((2, 32, 128), f32), pltpu.VMEM((64 * WY, 128), f32),
             pltpu.VMEM((6, 128, 128), f32), pltpu.VMEM((6, 128, 128), f32),
             pltpu.VMEM((2, 64, 128), f32), pltpu.VMEM((2, 64, 128), f32),
             pltpu.VMEM((1024, 512), bf16),
-            DMA, DMA, DMA((12,)), DMA((12,)), DMA((6,)), DMA((6,)), DMA((4,)), DMA((4,)),
+            DMA, DMA, DMA((12,)), DMA((12,)), DMA((6,)), DMA((6,)), DMA((4,)), DMA((4,)), pltpu.SemaphoreType.REGULAR,
         ],
-        compiler_params=pltpu.CompilerParams(vmem_limit_bytes=56 * 2**20, collective_id=0, has_side_effects=True),
+        compiler_params=pltpu.CompilerParams(vmem_limit_bytes=32 * 2**20, collective_id=0, has_side_effects=True),
         cost_estimate=pl.CostEstimate(flops=3_000_000_000, bytes_accessed=8_000_000, transcendentals=0),
         name="exchange",
     )(send, t, v, u, vv, w, cells, zed, heat)
@@ -484,7 +517,9 @@
     return hi, mid, (rest - mid.astype(f32)).astype(jnp.bfloat16)
 
 
-def compact_kernel(recv_ref, ro_ref, mo_ref, X):
+def compact_kernel(recv_ref, ti_ref, vi_ref, to_ref, vo_ref, ro_ref, mo_ref, X):
+    to_ref[...] = ti_ref[...]
+    vo_ref[...] = vi_ref[...]
     rows = []
     for g in range(8):
         rows.append(recv_ref[pl.ds(g * 128, 128), 128:256].T[0:1])
@@ -511,29 +546,19 @@
         mo_ref[pl.ds(n * 128, 128), :] = d[:, 128:256]
 
 
-def compacted(recv):
+def compacted(recv, t, v):
     VM = pl.BlockSpec(memory_space=pltpu.VMEM)
+    field = jax.ShapeDtypeStruct(t.shape, f32)
+    drops = jax.ShapeDtypeStruct((512, 128), f32)
     return pl.pallas_call(
         compact_kernel,
-        out_shape=(jax.ShapeDtypeStruct((512, 128), f32), jax.ShapeDtypeStruct((512, 128), f32)),
-        in_specs=[VM], out_specs=[VM, VM],
+        out_shape=(field, field, drops, drops),
+        in_specs=[VM] * 3, out_specs=[VM] * 4,
         scratch_shapes=[pltpu.VMEM((1024, 768), jnp.bfloat16)],
-        compiler_params=pltpu.CompilerParams(vmem_limit_bytes=16 * 2**20),
+        compiler_params=pltpu.CompilerParams(vmem_limit_bytes=12 * 2**20),
         cost_estimate=pl.CostEstimate(flops=800_000_000, bytes_accessed=2_000_000, transcendentals=0),
         name="compact",
-    )(recv)
-
-
-def selector(index, count):
-    return (jnp.arange(count, dtype=jnp.int32)[:, None] == index[None, :]).astype(jnp.float32)
-
-
-def select_rows(matrix, value):
-    flat = value.reshape((value.shape[0], -1))
-    picked = jnp.dot(
-        matrix, flat, precision=lax.Precision.HIGHEST, preferred_element_type=jnp.float32
-    )
-    return picked.reshape((matrix.shape[0],) + value.shape[1:])
+    )(recv, t, v)
 
 
 def body(
@@ -554,25 +579,21 @@
     columns = tprime.shape[0] * tprime.shape[1]
     levels = tprime.shape[2]
     flat = [a.reshape(columns, levels) for a in (tprime, vapor, wind_u, wind_v, wind_w)]
-    column_pick = selector(cell_index // levels, columns).T
-    level_pick = selector(cell_index % levels, levels).T
-    at_column = select_rows(column_pick, jnp.concatenate(flat[:2], axis=1))
-    cell_temp = jnp.sum(at_column[:, :levels] * level_pick, axis=1)
-    cell_vapor = jnp.sum(at_column[:, levels:] * level_pick, axis=1)
     square = (8, home // 8)
+    cells = cell_index.reshape(square)
     send, heat = physics(
+        cell_index,
+        flat[0],
+        flat[1],
         radius,
         min_radius,
         multiplicity,
         drop_counts.reshape(square),
-        cell_temp.reshape(square),
-        cell_vapor.reshape(square),
+        cells,
         move_list.reshape(1, home),
     )
-    temperature, humidity, recv = comm(
-        shape, send, *flat, cell_index.reshape(1, home), cell_index.reshape(square), heat
-    )
-    radius_out, multiplicity_out = compacted(recv)
+    temperature, humidity, recv = comm(shape, send, *flat, cell_index.reshape(1, home), cells, heat)
+    temperature, humidity, radius_out, multiplicity_out = compacted(recv, temperature, humidity)
     return (
         temperature.reshape(tprime.shape),
         humidity.reshape(vapor.shape),

time: 124 us -> 69.2 us (0.56)
  the two profiles are of different devices: /device:TPU:0 before, /device:TPU:1 now
where the time goes in v2:
time: 69.2 us; the launch traced here: 68.8 us
  Pallas kernels  61.8 us (89%)
  local copies, waits for them, and re-layouts  6.29 us (9%)
  between operations  0.73 us (1%)
    pallas_call x1, Pallas kernels, comm(): pl.pallas_call(functools.partial(comm_kernel, nx, ny), out_shape=(jax.Sha...  43.9 us
    pallas_call x1, Pallas kernels, physics(): pl.pallas_call(physics_kernel, out_shape=(jax.ShapeDtypeStruct((1024, 256...  15.2 us
    unnamed x26, local copies, waits for them, and re-layouts  6.29 us
    pallas_call x1, Pallas kernels, compacted(): pl.pallas_call(compact_kernel, out_shape=(field, field, drops, drops), in...  2.75 us

profile of v2, /device:TPU:1, one launch (start us, length us, event | category | flops | bytes accessed | tf_op | source)
XLA Modules:
  0.0 68.8 jit_solution(162773139876586315)
XLA Ops:
  0.6 0.0 copy-start.12
  0.6 0.0 copy-start.11
  0.7 0.0 copy-start.10
  0.7 0.7 copy-done.12
  1.3 0.0 copy-done.11
  1.3 0.0 copy-done.10
  1.4 0.0 copy-start
  1.4 1.2 %copy-done = f32[64,32,128]{2,1,0:T(8,128)S(1)} copy-done((f32[64,32,128]{2,1,0:T(8,128)S(1)}, f32[64,32,128]{2,1,0:T(8,128)}, u32[]{:S(2)}) %copy-start) | copy-done | bytes 1048600
  2.6 0.0 copy-start.2
  2.6 1.2 %copy-done.2 = f32[64,32,128]{2,1,0:T(8,128)S(1)} copy-done((f32[64,32,128]{2,1,0:T(8,128)S(1)}, f32[64,32,128]{2,1,0:T(8,128)}, u32[]{:S(2)}) %copy-start.2) | copy-done | bytes 1048600
  3.8 0.0 copy-start.7
  3.8 1.0 %copy-done.7 = f32[1024,128]{1,0:T(8,128)S(1)} copy-done((f32[1024,128]{1,0:T(8,128)S(1)}, f32[1024,128]{1,0:T(8,128)}, u32[]{:S(2)}) %copy-start.7) | copy-done | bytes 524312
  4.8 0.0 copy-start.8
  4.8 1.0 %copy-done.8 = f32[1024,128]{1,0:T(8,128)S(1)} copy-done((f32[1024,128]{1,0:T(8,128)S(1)}, f32[1024,128]{1,0:T(8,128)}, u32[]{:S(2)}) %copy-start.8) | copy-done | bytes 524312
  5.9 0.0 copy-start.9
  5.9 1.0 %copy-done.9 = f32[1024,128]{1,0:T(8,128)S(1)} copy-done((f32[1024,128]{1,0:T(8,128)S(1)}, f32[1024,128]{1,0:T(8,128)}, u32[]{:S(2)}) %copy-start.9) | copy-done | bytes 524312
  6.9 0.0 copy-start.1
  6.9 0.0 copy-start.3
  6.9 0.0 copy-start.4
  6.9 0.0 copy-start.5
  6.9 0.0 copy-start.6
  7.0 15.2 %physics.1 = (f32[1024,256]{1,0:T(8,128)S(1)}, f32[16,128]{1,0:T(8,128)S(1)}) custom-call(s32[1024]{0:T(1024)S(1)} %copy-done.12, f32[2048,128]{1,0:T(8,128)S(1)} %bitcast.11, f32[2048,128]{1,0:T(8,128)S(1)} %bitcast.13, f32[1024,128]{1,0:T(8,128)S(1)} %copy-done.7, f32[1024,128]{1,0:T(8,128)S(1)} %copy-done.8, f32[1024,128]{1,0:T(8,128)S(1)} %copy-done.9, ...), custom_call_target="tpu_custom_call" | custom-call | flops 1700000000 | bytes 3000000 | tf_op jit(solution)/shard_map/physics/pallas_call | solution.py:284
  22.2 0.0 copy-done.1
  22.2 0.0 copy-done.3
  22.2 0.0 copy-done.4
  22.2 0.0 copy-done.5
  22.2 0.0 copy-done.6
  22.2 43.9 %exchange.1 = (f32[2048,128]{1,0:T(8,128)S(1)}, f32[2048,128]{1,0:T(8,128)S(1)}, f32[1024,256]{1,0:T(8,128)S(1)}) custom-call(f32[1024,256]{1,0:T(8,128)S(1)} %get-tuple-element.13.send_ref, f32[2048,128]{1,0:T(8,128)S(1)} %bitcast.12, f32[2048,128]{1,0:T(8,128)S(1)} %bitcast.14, f32[2048,128]{1,0:T(8,128)S(1)} %bitcast.15, f32[2048,128]{1,0:T(8,128)S(1)} %bitcast.16, ...), custom_call_target="tpu_custom_call" | custom-call | flops 3000000000 | bytes 8000000 | tf_op jit(solution)/shard_map/exchange/pallas_call | solution.py:489
  66.1 2.7 %compact.1 = (f32[2048,128]{1,0:T(8,128)}, f32[2048,128]{1,0:T(8,128)}, f32[512,128]{1,0:T(8,128)}, f32[512,128]{1,0:T(8,128)}) custom-call(f32[1024,256]{1,0:T(8,128)S(1)} %get-tuple-element.15.recv_ref, f32[2048,128]{1,0:T(8,128)S(1)} %get-tuple-element.16.ti_ref, f32[2048,128]{1,0:T(8,128)S(1)} %get-tuple-element.17.vi_ref), custom_call_target="tpu_custom_call" | custom-call | flops 800000000 | bytes 2000000 | tf_op jit(solution)/shard_map/compact/pallas_call | solution.py:553
Async XLA Ops:
  0.6 0.7 copy-start.12
  0.6 0.7 %copy-start.11 = (s32[1024]{0:T(1024)S(1)}, s32[1024]{0:T(1024)}, u32[]{:S(2)}) copy-start(s32[1024]{0:T(1024)} %param.21) | copy-start | bytes 12292
  0.7 0.7 %copy-start.10 = (s32[1024]{0:T(1024)S(1)}, s32[1024]{0:T(1024)}, u32[]{:S(2)}) copy-start(s32[1024]{0:T(1024)} %param.19) | copy-start | bytes 12292
  1.4 1.2 %copy-start = (f32[64,32,128]{2,1,0:T(8,128)S(1)}, f32[64,32,128]{2,1,0:T(8,128)}, u32[]{:S(2)}) copy-start(f32[64,32,128]{2,1,0:T(8,128)} %param.11) | copy-start | bytes 3145732
  2.6 1.2 %copy-start.2 = (f32[64,32,128]{2,1,0:T(8,128)S(1)}, f32[64,32,128]{2,1,0:T(8,128)}, u32[]{:S(2)}) copy-start(f32[64,32,128]{2,1,0:T(8,128)} %param.12) | copy-start | bytes 3145732
  3.8 1.0 %copy-start.7 = (f32[1024,128]{1,0:T(8,128)S(1)}, f32[1024,128]{1,0:T(8,128)}, u32[]{:S(2)}) copy-start(f32[1024,128]{1,0:T(8,128)} %rad_ref.1) | copy-start | bytes 1572868
  4.8 1.0 %copy-start.8 = (f32[1024,128]{1,0:T(8,128)S(1)}, f32[1024,128]{1,0:T(8,128)}, u32[]{:S(2)}) copy-start(f32[1024,128]{1,0:T(8,128)} %flo_ref.1) | copy-start | bytes 1572868
  5.9 1.0 %copy-start.9 = (f32[1024,128]{1,0:T(8,128)S(1)}, f32[1024,128]{1,0:T(8,128)}, u32[]{:S(2)}) copy-start(f32[1024,128]{1,0:T(8,128)} %mul_ref.1) | copy-start | bytes 1572868
  6.9 15.2 %copy-start.1 = (f32[64,32,128]{2,1,0:T(8,128)S(1)}, f32[64,32,128]{2,1,0:T(8,128)}, u32[]{:S(2)}) copy-start(f32[64,32,128]{2,1,0:T(8,128)} %param.11) | copy-start | bytes 3145732
  6.9 15.2 %copy-start.3 = (f32[64,32,128]{2,1,0:T(8,128)S(1)}, f32[64,32,128]{2,1,0:T(8,128)}, u32[]{:S(2)}) copy-start(f32[64,32,128]{2,1,0:T(8,128)} %param.12) | copy-start | bytes 3145732
  6.9 15.2 %copy-start.4 = (f32[64,32,128]{2,1,0:T(8,128)S(1)}, f32[64,32,128]{2,1,0:T(8,128)}, u32[]{:S(2)}) copy-start(f32[64,32,128]{2,1,0:T(8,128)} %param.13) | copy-start | bytes 3145732
  6.9 15.2 %copy-start.5 = (f32[64,32,128]{2,1,0:T(8,128)S(1)}, f32[64,32,128]{2,1,0:T(8,128)}, u32[]{:S(2)}) copy-start(f32[64,32,128]{2,1,0:T(8,128)} %param.14) | copy-start | bytes 3145732
  6.9 15.2 %copy-start.6 = (f32[64,32,128]{2,1,0:T(8,128)S(1)}, f32[64,32,128]{2,1,0:T(8,128)}, u32[]{:S(2)}) copy-start(f32[64,32,128]{2,1,0:T(8,128)} %param.15) | copy-start | bytes 3145732

commit v3 on v2

--- a/solution.py
+++ b/solution.py
@@ -12,6 +12,7 @@
 SUBSTEPS = 6
 WX, WY = 66, 48
 UNROLL = 8
+EARLY, SECOND = 3, 6
 
 clausius = 0.07
 growth = 200.0 / 3.0
@@ -164,15 +165,13 @@
             cell[pl.ds(g, 1), :] = jnp.sum(picked, axis=0, keepdims=True)
 
 
-def physics_kernel(index, t_ref, v_ref, rad_ref, flo_ref, mul_ref, cnt_ref, cell_ref, move_ref, send_ref, heat_ref, R, S, C, F, M, marks, X, ct_ref, cv_ref):
-    gather_cells(index, t_ref, v_ref, cell_ref, ct_ref, cv_ref, S, C)
+def condense_blocks(rad_ref, flo_ref, mul_ref, cnt_ref, heat_ref, R, S, C, F, M, ct_ref, cv_ref):
 
     def enter(g, c):
-        at = pl.ds(pl.multiple_of(g * 128, 128), 128)
         to = pl.ds(g, 128, stride=8)
-        R[to, :] = rad_ref[at, :].T
-        F[to, :] = flo_ref[at, :].T
-        M[to, :] = mul_ref[at, :].T
+        R[to, :] = rad_ref[g].T
+        F[to, :] = flo_ref[g].T
+        M[to, :] = mul_ref[g].T
         return c
     lax.fori_loop(0, 8, enter, 0)
     counts = cnt_ref[...]
@@ -218,6 +217,11 @@
     heat_ref[0:8, :] = temp - ct_ref[...]
     heat_ref[8:16, :] = wet - cv_ref[...]
 
+
+def collect_blocks(R, S, C, F, M, marks, X):
+    zero = jnp.zeros((8, 128), jnp.float32)
+    U = 8
+
     def radii(t, c):
         for u in range(U):
             d = t * U + u
@@ -267,30 +271,6 @@
                 X[at, k * 256 + q * 128:k * 256 + q * 128 + 128] = part
         return c
     lax.fori_loop(0, 8, leave, 0)
-    moves_to = move_ref[...]
-
-    def place(n, c):
-        at = pl.multiple_of(n * 128, 128)
-        ids = lax.broadcasted_iota(jnp.int32, (128, 1024), 0) + at
-        hot = jnp.where(ids == moves_to, 1.0, 0.0).astype(jnp.bfloat16)
-        d = jnp.dot(hot, X[...], preferred_element_type=f32)
-        send_ref[pl.ds(at, 128), :] = d[:, 0:256] + (d[:, 256:512] + d[:, 512:768])
-        return c
-    lax.fori_loop(0, 8, place, 0)
-
-
-def physics(index, t, v, radius, floor_radius, mult, counts, cells, move_list):
-    VM = pl.BlockSpec(memory_space=pltpu.VMEM)
-    return pl.pallas_call(
-        physics_kernel,
-        out_shape=(jax.ShapeDtypeStruct((1024, 256), f32), jax.ShapeDtypeStruct((16, 128), f32)),
-        in_specs=[pl.BlockSpec(memory_space=pltpu.SMEM)] + [VM] * 8,
-        out_specs=[VM] * 2,
-        scratch_shapes=[pltpu.VMEM((1024, 128), f32)] * 5 + [pltpu.VMEM((N_CE * 8, 128), f32), pltpu.VMEM((1024, 768), jnp.bfloat16), pltpu.VMEM((8, 128), f32), pltpu.VMEM((8, 128), f32)],
-        compiler_params=pltpu.CompilerParams(vmem_limit_bytes=20 * 2**20),
-        cost_estimate=pl.CostEstimate(flops=1_700_000_000, bytes_accessed=3_000_000, transcendentals=1_000_000),
-        name="physics",
-    )(index, t, v, radius, floor_radius, mult, counts, cells, move_list)
 
 
 def mod(a, n):
@@ -303,32 +283,59 @@
     return hi, lo
 
 
-def comm_kernel(nx, ny, send_ref, t_ref, v_ref, u_ref, vv_ref, w_ref, cell_ref, zed_ref, heat_ref,
+def row_moves(nx, ny, ix, iy, k, send_ref, recv_ref, s, r):
+    px = mod(ix + k, nx)
+    me = ix * ny + iy
+
+    def body(i, c):
+        py = mod(iy + i, ny)
+        pltpu.make_async_remote_copy(
+            src_ref=send_ref.at[pl.ds(pl.multiple_of((px * ny + py) * 8, 8), 8), :],
+            dst_ref=recv_ref.at[pl.ds(pl.multiple_of(me * 8, 8), 8), :],
+            send_sem=s, recv_sem=r, device_id=(px, py), device_id_type=MESH).start()
+        return c
+    lax.fori_loop(1 if k == 0 else 0, ny, body, 0)
+
+
+def step_kernel(nx, ny, index, t_hbm, v_hbm, u_hbm, vv_hbm, w_hbm, rad_hbm, flo_hbm, mul_hbm, cnt_ref, square_ref, cell_ref, move_ref,
                 to_ref, vo_ref, recv_ref,
-                E, AX, AL, AH, AZ, AD, UE, VE, yout, yin, vout, vin, W,
-                a2a_send, a2a_recv, xs, xr, ys, yr, ws, wr, rows):
+                t_ref, v_ref, u_ref, vv_ref, w_ref, rad_ref, flo_ref, mul_ref, send_ref, heat_ref, R, S, C, F, M, marks, X, ct_ref, cv_ref,
+                E, AX, AL, AH, AZ, AD, UE, VE, xin, yout, yin, vout, vin, W,
+                a2a_send, a2a_recv, xs, xr, ys, yr, ws, wr, rows, loads):
     ix, iy = lax.axis_index("gx"), lax.axis_index("gy")
     me = ix * ny + iy
-    count = nx * ny
     right, left = (mod(ix + 1, nx), iy), (mod(ix - 1, nx), iy)
     upper, lower = (ix, mod(iy + 1, ny)), (ix, mod(iy - 1, ny))
 
+    fetched = []
+    for n, (src, dst) in enumerate(((t_hbm, t_ref), (v_hbm, v_ref), (rad_hbm, rad_ref), (flo_hbm, flo_ref), (mul_hbm, mul_ref), (vv_hbm, vv_ref), (u_hbm, u_ref), (w_hbm, w_ref))):
+        fetched.append(pltpu.make_async_copy(src, dst, loads.at[n]))
+        fetched[-1].start()
     barrier = pltpu.get_barrier_semaphore()
-
     for i in range(1, ny):
         pl.semaphore_signal(barrier, inc=1, device_id=(ix, mod(iy + i, ny)), device_id_type=MESH)
     for i in range(1, nx):
         pl.semaphore_signal(barrier, inc=1, device_id=(mod(ix + i, nx), iy), device_id_type=MESH)
 
+    def remote(src, dst, s, r, to):
+        return pltpu.make_async_remote_copy(src_ref=src, dst_ref=dst, send_sem=s, recv_sem=r, device_id=to, device_id_type=MESH)
+
+    fetched[0].wait()
+    fetched[1].wait()
+    gather_cells(index, t_ref, v_ref, square_ref, ct_ref, cv_ref, S, C)
+    for n in (2, 3, 4):
+        fetched[n].wait()
+    condense_blocks(rad_ref, flo_ref, mul_ref, cnt_ref, heat_ref, R, S, C, F, M, ct_ref, cv_ref)
+    fetched[5].wait()
+    fetched[6].wait()
     vout[0] = vv_ref[pl.ds(31, 64, stride=32), :]
     vout[1] = vv_ref[pl.ds(0, 64, stride=32), :]
+    for e in range(6):
+        for at in (WY + 7, WY + 40):
+            E[e, pl.ds(at, 64, stride=WY), :] = jnp.zeros((64, 128), f32)
     pl.semaphore_wait(barrier, nx + ny - 2)
     for i in range(1, ny):
         pl.semaphore_signal(rows, inc=1, device_id=(ix, mod(iy + i, ny)), device_id_type=MESH)
-
-    def remote(src, dst, s, r, to):
-        return pltpu.make_async_remote_copy(src_ref=src, dst_ref=dst, send_sem=s, recv_sem=r, device_id=to, device_id_type=MESH)
-
     winds = [
         remote(u_ref.at[pl.ds(63 * 32, 32), :], UE.at[0], ws.at[0], wr.at[0], right),
         remote(u_ref.at[pl.ds(0, 32), :], UE.at[1], ws.at[1], wr.at[1], left),
@@ -337,26 +344,30 @@
     ]
     for c in winds:
         c.start()
-
-    def chunk(i):
-        p = mod(me + i, count)
-        return remote(
-            send_ref.at[pl.ds(pl.multiple_of(p * 8, 8), 8), :],
-            recv_ref.at[pl.ds(pl.multiple_of(me * 8, 8), 8), :],
-            a2a_send, a2a_recv, (p // ny, lax.rem(p, ny)))
-
-    def send_some(lo, hi):
-        def body(i, c):
-            chunk(i).start()
-            return c
-        lax.fori_loop(lo, hi, body, 0)
-
+    collect_blocks(R, S, C, F, M, marks, X)
+    moves_to = move_ref[...]
+
+    def place(k):
+        at = pl.multiple_of(mod(ix + k, nx) * (ny * 8), ny * 8)
+        ids = lax.broadcasted_iota(jnp.int32, (ny * 8, 1024), 0) + at
+        hot = jnp.where(ids == moves_to, 1.0, 0.0).astype(jnp.bfloat16)
+        d = jnp.dot(hot, X[...], preferred_element_type=f32)
+        send_ref[pl.ds(at, ny * 8), :] = d[:, 0:256] + (d[:, 256:512] + d[:, 512:768])
+
+    def send_row(k):
+        row_moves(nx, ny, ix, iy, k, send_ref, recv_ref, a2a_send, a2a_recv)
+
+    place(0)
     pl.semaphore_wait(rows, ny - 1)
-    send_some(1, count // 3)
+    send_row(0)
+    for k in range(1, nx):
+        place(k)
+        if k < EARLY:
+            send_row(k)
     mine = pl.ds(pl.multiple_of(me * 8, 8), 8)
     recv_ref[mine, :] = send_ref[mine, :]
 
-    zed = lax.rem(zed_ref[...], 128).astype(f32).T.astype(jnp.int32)
+    zed = lax.rem(square_ref[...], 128).astype(f32).T.astype(jnp.int32)
     heat = heat_ref[...].T
     lanes = lax.broadcasted_iota(jnp.int32, (128, 128), 1)
     for g in range(8):
@@ -389,8 +400,9 @@
         moves = []
         for q in range(2):
             e = E.at[2 * s + q]
-            moves.append(remote(e.at[pl.ds(plane(64), 32), :], e.at[pl.ds(plane(0), 32), :], xs.at[4 * s + 2 * q], xr.at[4 * s + 2 * q], right))
-            moves.append(remote(e.at[pl.ds(plane(1), 32), :], e.at[pl.ds(plane(65), 32), :], xs.at[4 * s + 2 * q + 1], xr.at[4 * s + 2 * q + 1], left))
+            n = 4 * s + 2 * q
+            moves.append(remote(e.at[pl.ds(plane(64), 32), :], xin.at[n], xs.at[n], xr.at[n], right))
+            moves.append(remote(e.at[pl.ds(plane(1), 32), :], xin.at[n + 1], xs.at[n + 1], xr.at[n + 1], left))
             yout[2 * s, pl.ds(64 * q, 64), :] = E[2 * s + q, pl.ds(plane(1) + 31, 64, stride=WY), :]
             yout[2 * s + 1, pl.ds(64 * q, 64), :] = E[2 * s + q, pl.ds(plane(1), 64, stride=WY), :]
         moves.append(remote(yout.at[2 * s], yin.at[2 * s], ys.at[2 * s], yr.at[2 * s], upper))
@@ -399,15 +411,10 @@
             c.start()
         return moves
 
-    def arrive(s, moves):
-        for c in moves:
-            c.wait_recv()
-        for q in range(2):
-            E[2 * s + q, pl.ds(plane(1) - 1, 64, stride=WY), :] = yin[2 * s, pl.ds(64 * q, 64), :]
-            E[2 * s + q, pl.ds(plane(1) + 32, 64, stride=WY), :] = yin[2 * s + 1, pl.ds(64 * q, 64), :]
-
     moves = exchange(0)
-    send_some(count // 3, 2 * count // 3)
+    for k in range(EARLY, SECOND):
+        send_row(k)
+    fetched[7].wait()
     for c in winds:
         c.wait_recv()
 
@@ -445,7 +452,6 @@
     lax.fori_loop(0, 9, face_x, 0)
 
     for s, weight in enumerate((advect_step / 3.0, advect_step / 2.0, advect_step)):
-        arrive(s, moves)
         for q in range(2):
             src = E.at[2 * s + q]
             start = E.at[q]
@@ -467,43 +473,62 @@
                     f, low = after, high
                 return f, low
             f0 = src[pl.ds(plane(1), 32), :]
-            lax.fori_loop(0, 64 // UNROLL, step, (f0, AX[pl.ds(0, 32), :] * (src[pl.ds(plane(0), 32), :] + f0)))
+            lax.fori_loop(0, 64 // UNROLL, step, (f0, AX[pl.ds(0, 32), :] * f0))
+        for c in moves:
+            c.wait_recv()
+        for q in range(2):
+            if s < 2:
+                dst, base, wide = E.at[2 * s + 2 + q], plane(1), WY
+            else:
+                dst, base, wide = (to_ref, vo_ref)[q], 0, 32
+            n = 4 * s + 2 * q
+            first, last = pl.ds(base, 32), pl.ds(base + 63 * wide, 32)
+            dst[first, :] = dst[first, :] + weight * (AX[pl.ds(0, 32), :] * xin[n])
+            dst[last, :] = dst[last, :] - weight * (AX[pl.ds(64 * 32, 32), :] * xin[n + 1])
+            bottom, top = pl.ds(base, 64, stride=wide), pl.ds(base + 31, 64, stride=wide)
+            dst[bottom, :] = dst[bottom, :] + weight * (AL[pl.ds(0, 64, stride=32), :] * yin[2 * s, pl.ds(64 * q, 64), :])
+            dst[top, :] = dst[top, :] - weight * (AH[pl.ds(31, 64, stride=32), :] * yin[2 * s + 1, pl.ds(64 * q, 64), :])
         for c in moves:
             c.wait_send()
         if s < 2:
             moves = exchange(s + 1)
         if s == 0:
-            send_some(2 * count // 3, count)
+            for k in range(SECOND, nx):
+                send_row(k)
     for c in winds:
         c.wait_send()
-    whole = remote(recv_ref.at[pl.ds(8, 8 * (count - 1)), :], recv_ref.at[pl.ds(8, 8 * (count - 1)), :], a2a_send, a2a_recv, right)
+    rest = pl.ds(8, 8 * (nx * ny - 1))
+    whole = remote(recv_ref.at[rest, :], recv_ref.at[rest, :], a2a_send, a2a_recv, right)
     whole.wait_send()
     whole.wait_recv()
 
 
-def comm(mesh_shape, send, t, v, u, vv, w, cells, zed, heat):
+def step_call(mesh_shape, index, fields, droplets, counts, square, cells, moves):
     nx, ny = mesh_shape
     VM = pl.BlockSpec(memory_space=pltpu.VMEM)
+    HB = pl.BlockSpec(memory_space=pltpu.HBM)
     bf16 = jnp.bfloat16
     DMA = pltpu.SemaphoreType.DMA
+    plane = pltpu.VMEM((2048, 128), f32)
+    block = pltpu.VMEM((1024, 128), f32)
     return pl.pallas_call(
-        functools.partial(comm_kernel, nx, ny),
+        functools.partial(step_kernel, nx, ny),
         out_shape=(jax.ShapeDtypeStruct((2048, 128), f32), jax.ShapeDtypeStruct((2048, 128), f32), jax.ShapeDtypeStruct((1024, 256), f32)),
-        in_specs=[VM] * 9,
+        in_specs=[pl.BlockSpec(memory_space=pltpu.SMEM)] + [HB] * 8 + [VM] * 4,
         out_specs=[VM] * 3,
-        scratch_shapes=[
-            pltpu.VMEM((6, WX * WY, 128), f32),
-            pltpu.VMEM((65 * 32, 128), f32), pltpu.VMEM((2048, 128), f32), pltpu.VMEM((2048, 128), f32), pltpu.VMEM((2048, 128), f32), pltpu.VMEM((2048, 128), f32),
+        scratch_shapes=[plane] * 5 + [pltpu.VMEM((8, 128, 128), f32)] * 3 + [pltpu.VMEM((1024, 256), f32), pltpu.VMEM((16, 128), f32)] + [block] * 5
+        + [pltpu.VMEM((N_CE * 8, 128), f32), pltpu.VMEM((1024, 768), bf16), pltpu.VMEM((8, 128), f32), pltpu.VMEM((8, 128), f32)]
+        + [
+            pltpu.VMEM((6, WX * WY, 128), f32), pltpu.VMEM((65 * 32, 128), f32), plane, plane, plane, plane,
             pltpu.VMEM((2, 32, 128), f32), pltpu.VMEM((64 * WY, 128), f32),
-            pltpu.VMEM((6, 128, 128), f32), pltpu.VMEM((6, 128, 128), f32),
-            pltpu.VMEM((2, 64, 128), f32), pltpu.VMEM((2, 64, 128), f32),
-            pltpu.VMEM((1024, 512), bf16),
-            DMA, DMA, DMA((12,)), DMA((12,)), DMA((6,)), DMA((6,)), DMA((4,)), DMA((4,)), pltpu.SemaphoreType.REGULAR,
+            pltpu.VMEM((12, 32, 128), f32), pltpu.VMEM((6, 128, 128), f32), pltpu.VMEM((6, 128, 128), f32),
+            pltpu.VMEM((2, 64, 128), f32), pltpu.VMEM((2, 64, 128), f32), pltpu.VMEM((1024, 512), bf16),
+            DMA, DMA, DMA((12,)), DMA((12,)), DMA((6,)), DMA((6,)), DMA((4,)), DMA((4,)), pltpu.SemaphoreType.REGULAR, DMA((8,)),
         ],
-        compiler_params=pltpu.CompilerParams(vmem_limit_bytes=32 * 2**20, collective_id=0, has_side_effects=True),
-        cost_estimate=pl.CostEstimate(flops=3_000_000_000, bytes_accessed=8_000_000, transcendentals=0),
-        name="exchange",
-    )(send, t, v, u, vv, w, cells, zed, heat)
+        compiler_params=pltpu.CompilerParams(vmem_limit_bytes=50 * 2**20, collective_id=0, has_side_effects=True),
+        cost_estimate=pl.CostEstimate(flops=5_000_000_000, bytes_accessed=8_000_000, transcendentals=0),
+        name="step",
+    )(index, *fields, *droplets, counts, square, cells, moves)
 
 
 def triangle(n):
@@ -578,21 +603,19 @@
     home = radius.shape[0]
     columns = tprime.shape[0] * tprime.shape[1]
     levels = tprime.shape[2]
-    flat = [a.reshape(columns, levels) for a in (tprime, vapor, wind_u, wind_v, wind_w)]
+    flat = [pltpu.with_memory_space_constraint(a.reshape(columns, levels), pltpu.HBM) for a in (tprime, vapor, wind_u, wind_v, wind_w)]
     square = (8, home // 8)
     cells = cell_index.reshape(square)
-    send, heat = physics(
+    temperature, humidity, recv = step_call(
+        shape,
         cell_index,
-        flat[0],
-        flat[1],
-        radius,
-        min_radius,
-        multiplicity,
+        flat,
+        [pltpu.with_memory_space_constraint(a.reshape(8, home // 8, a.shape[1]), pltpu.HBM) for a in (radius, min_radius, multiplicity)],
         drop_counts.reshape(square),
         cells,
+        cell_index.reshape(1, home),
         move_list.reshape(1, home),
     )
-    temperature, humidity, recv = comm(shape, send, *flat, cell_index.reshape(1, home), cells, heat)
     temperature, humidity, radius_out, multiplicity_out = compacted(recv, temperature, humidity)
     return (
         temperature.reshape(tprime.shape),

time: 69.2 us -> 53.7 us (0.78)
  Pallas kernels: 61.8 us -> 52.1 us
  local copies, waits for them, and re-layouts: 6.29 us -> 0.7 us
    pallas_call x2 -> x1, Pallas kernels: 59.1 us -> 49.4 us  [step_call(): pl.pallas_call(functools.partial(step_kernel, nx, ny), out_shape=(jax.Sha...]
    unnamed x26 -> x6, local copies, waits for them, and re-layouts: 6.29 us -> 0.7 us
where the time goes in v3:
time: 53.7 us; the launch traced here: 53.5 us
  Pallas kernels  52.1 us (97%)
  local copies, waits for them, and re-layouts  0.7 us (1%)
  between operations  0.67 us (1%)
    pallas_call x1, Pallas kernels, step_call(): pl.pallas_call(functools.partial(step_kernel, nx, ny), out_shape=(jax.Sha...  49.4 us
    pallas_call x1, Pallas kernels, compacted(): pl.pallas_call(compact_kernel, out_shape=(field, field, drops, drops), in...  2.75 us

profile of v3, /device:TPU:1, one launch (start us, length us, event | category | flops | bytes accessed | tf_op | source)
XLA Modules:
  0.0 53.5 jit_solution(8063662670193283705)
XLA Ops:
  0.6 0.0 copy-start.2
  0.6 0.0 copy-start.1
  0.7 0.0 copy-start
  0.7 0.7 %copy-done.2 = s32[1024]{0:T(1024)S(1)} copy-done((s32[1024]{0:T(1024)S(1)}, s32[1024]{0:T(1024)}, u32[]{:S(2)}) %copy-start.2) | copy-done | bytes 4120
  1.3 0.0 copy-done.1
  1.3 0.0 copy-done
  1.4 49.4 %step.1 = (f32[2048,128]{1,0:T(8,128)S(1)}, f32[2048,128]{1,0:T(8,128)S(1)}, f32[1024,256]{1,0:T(8,128)S(1)}) custom-call(s32[1024]{0:T(1024)S(1)} %copy-done, f32[2048,128]{1,0:T(8,128)} %bitcast.18, f32[2048,128]{1,0:T(8,128)} %bitcast.19, f32[2048,128]{1,0:T(8,128)} %bitcast.20, f32[2048,128]{1,0:T(8,128)} %bitcast.21, f32[2048,128]{1,0:T(8,128)} %bitcast.22, ...), custom_call_target="tpu_custom_call" | custom-call | flops 5000000000 | bytes 8000000 | tf_op jit(solution)/shard_map/step/pallas_call | solution.py:514
  50.8 2.7 %compact.1 = (f32[2048,128]{1,0:T(8,128)}, f32[2048,128]{1,0:T(8,128)}, f32[512,128]{1,0:T(8,128)}, f32[512,128]{1,0:T(8,128)}) custom-call(f32[1024,256]{1,0:T(8,128)S(1)} %get-tuple-element.11.recv_ref, f32[2048,128]{1,0:T(8,128)S(1)} %get-tuple-element.12.ti_ref, f32[2048,128]{1,0:T(8,128)S(1)} %get-tuple-element.13.vi_ref), custom_call_target="tpu_custom_call" | custom-call | flops 800000000 | bytes 2000000 | tf_op jit(solution)/shard_map/compact/pallas_call | solution.py:578
Async XLA Ops:
  0.6 0.7 %copy-start.2 = (s32[1024]{0:T(1024)S(1)}, s32[1024]{0:T(1024)}, u32[]{:S(2)}) copy-start(s32[1024]{0:T(1024)} %param.21) | copy-start | bytes 12292
  0.6 0.7 %copy-start.1 = (s32[1024]{0:T(1024)S(1)}, s32[1024]{0:T(1024)}, u32[]{:S(2)}) copy-start(s32[1024]{0:T(1024)} %param.19) | copy-start | bytes 12292
  0.7 0.7 %copy-start = (s32[1024]{0:T(1024)S(1)}, s32[1024]{0:T(1024)}, u32[]{:S(2)}) copy-start(s32[1024]{0:T(1024)} %index.1) | copy-start | bytes 12292

commit v4 on v3

--- a/solution.py
+++ b/solution.py
@@ -12,7 +12,6 @@
 SUBSTEPS = 6
 WX, WY = 66, 48
 UNROLL = 8
-EARLY, SECOND = 3, 6
 
 clausius = 0.07
 growth = 200.0 / 3.0
@@ -176,7 +175,7 @@
     lax.fori_loop(0, 8, enter, 0)
     counts = cnt_ref[...]
     zero = jnp.zeros((8, 128), jnp.float32)
-    U = 8
+    U = 32
 
     def init(t, w):
         for u in range(U):
@@ -220,7 +219,7 @@
 
 def collect_blocks(R, S, C, F, M, marks, X):
     zero = jnp.zeros((8, 128), jnp.float32)
-    U = 8
+    U = 16
 
     def radii(t, c):
         for u in range(U):
@@ -267,7 +266,7 @@
         at = pl.ds(pl.multiple_of(g * 128, 128), 128)
         frm = pl.ds(g, 128, stride=8)
         for q, ref in enumerate((S, C)):
-            for k, part in enumerate(split3(ref[frm, :].T)):
+            for k, part in enumerate(split2(ref[frm, :].T)):
                 X[at, k * 256 + q * 128:k * 256 + q * 128 + 128] = part
         return c
     lax.fori_loop(0, 8, leave, 0)
@@ -333,6 +332,7 @@
     for e in range(6):
         for at in (WY + 7, WY + 40):
             E[e, pl.ds(at, 64, stride=WY), :] = jnp.zeros((64, 128), f32)
+        E[e, pl.ds(65 * WY + 8, 32), :] = jnp.zeros((32, 128), f32)
     pl.semaphore_wait(barrier, nx + ny - 2)
     for i in range(1, ny):
         pl.semaphore_signal(rows, inc=1, device_id=(ix, mod(iy + i, ny)), device_id_type=MESH)
@@ -344,29 +344,6 @@
     ]
     for c in winds:
         c.start()
-    collect_blocks(R, S, C, F, M, marks, X)
-    moves_to = move_ref[...]
-
-    def place(k):
-        at = pl.multiple_of(mod(ix + k, nx) * (ny * 8), ny * 8)
-        ids = lax.broadcasted_iota(jnp.int32, (ny * 8, 1024), 0) + at
-        hot = jnp.where(ids == moves_to, 1.0, 0.0).astype(jnp.bfloat16)
-        d = jnp.dot(hot, X[...], preferred_element_type=f32)
-        send_ref[pl.ds(at, ny * 8), :] = d[:, 0:256] + (d[:, 256:512] + d[:, 512:768])
-
-    def send_row(k):
-        row_moves(nx, ny, ix, iy, k, send_ref, recv_ref, a2a_send, a2a_recv)
-
-    place(0)
-    pl.semaphore_wait(rows, ny - 1)
-    send_row(0)
-    for k in range(1, nx):
-        place(k)
-        if k < EARLY:
-            send_row(k)
-    mine = pl.ds(pl.multiple_of(me * 8, 8), 8)
-    recv_ref[mine, :] = send_ref[mine, :]
-
     zed = lax.rem(square_ref[...], 128).astype(f32).T.astype(jnp.int32)
     heat = heat_ref[...].T
     lanes = lax.broadcasted_iota(jnp.int32, (128, 128), 1)
@@ -396,24 +373,45 @@
     def plane(x):
         return x * WY + 8
 
-    def exchange(s):
-        moves = []
-        for q in range(2):
-            e = E.at[2 * s + q]
-            n = 4 * s + 2 * q
-            moves.append(remote(e.at[pl.ds(plane(64), 32), :], xin.at[n], xs.at[n], xr.at[n], right))
-            moves.append(remote(e.at[pl.ds(plane(1), 32), :], xin.at[n + 1], xs.at[n + 1], xr.at[n + 1], left))
-            yout[2 * s, pl.ds(64 * q, 64), :] = E[2 * s + q, pl.ds(plane(1) + 31, 64, stride=WY), :]
-            yout[2 * s + 1, pl.ds(64 * q, 64), :] = E[2 * s + q, pl.ds(plane(1), 64, stride=WY), :]
-        moves.append(remote(yout.at[2 * s], yin.at[2 * s], ys.at[2 * s], yr.at[2 * s], upper))
-        moves.append(remote(yout.at[2 * s + 1], yin.at[2 * s + 1], ys.at[2 * s + 1], yr.at[2 * s + 1], lower))
+    def exchange(s, q):
+        n = 4 * s + 2 * q
+        e = E.at[2 * s + q]
+        yout[n] = E[2 * s + q, pl.ds(plane(1) + 31, 64, stride=WY), :]
+        yout[n + 1] = E[2 * s + q, pl.ds(plane(1), 64, stride=WY), :]
+        moves = [
+            remote(yout.at[n], yin.at[n], ys.at[n], yr.at[n], upper),
+            remote(yout.at[n + 1], yin.at[n + 1], ys.at[n + 1], yr.at[n + 1], lower),
+            remote(e.at[pl.ds(plane(64), 32), :], xin.at[n], xs.at[n], xr.at[n], right),
+            remote(e.at[pl.ds(plane(1), 32), :], xin.at[n + 1], xs.at[n + 1], xr.at[n + 1], left),
+        ]
         for c in moves:
             c.start()
         return moves
 
-    moves = exchange(0)
-    for k in range(EARLY, SECOND):
+    moves = [exchange(0, 0), exchange(0, 1)]
+    sent = [*winds, *moves[0], *moves[1]]
+    collect_blocks(R, S, C, F, M, marks, X)
+    moves_to = move_ref[...]
+
+    def place(k):
+        at = pl.multiple_of(mod(ix + k, nx) * (ny * 8), ny * 8)
+        ids = lax.broadcasted_iota(jnp.int32, (ny * 8, 1024), 0) + at
+        hot = jnp.where(ids == moves_to, 1.0, 0.0).astype(jnp.bfloat16)
+        d = jnp.dot(hot, X[...], preferred_element_type=f32)
+        send_ref[pl.ds(at, ny * 8), :] = d[:, 0:256] + d[:, 256:512]
+
+    def send_row(k):
+        row_moves(nx, ny, ix, iy, k, send_ref, recv_ref, a2a_send, a2a_recv)
+
+    place(0)
+    pl.semaphore_wait(rows, ny - 1)
+    send_row(0)
+    for k in range(1, nx):
+        place(k)
         send_row(k)
+    mine = pl.ds(pl.multiple_of(me * 8, 8), 8)
+    recv_ref[mine, :] = send_ref[mine, :]
+
     fetched[7].wait()
     for c in winds:
         c.wait_recv()
@@ -474,9 +472,8 @@
                 return f, low
             f0 = src[pl.ds(plane(1), 32), :]
             lax.fori_loop(0, 64 // UNROLL, step, (f0, AX[pl.ds(0, 32), :] * f0))
-        for c in moves:
-            c.wait_recv()
-        for q in range(2):
+            for c in moves[q]:
+                c.wait_recv()
             if s < 2:
                 dst, base, wide = E.at[2 * s + 2 + q], plane(1), WY
             else:
@@ -486,16 +483,12 @@
             dst[first, :] = dst[first, :] + weight * (AX[pl.ds(0, 32), :] * xin[n])
             dst[last, :] = dst[last, :] - weight * (AX[pl.ds(64 * 32, 32), :] * xin[n + 1])
             bottom, top = pl.ds(base, 64, stride=wide), pl.ds(base + 31, 64, stride=wide)
-            dst[bottom, :] = dst[bottom, :] + weight * (AL[pl.ds(0, 64, stride=32), :] * yin[2 * s, pl.ds(64 * q, 64), :])
-            dst[top, :] = dst[top, :] - weight * (AH[pl.ds(31, 64, stride=32), :] * yin[2 * s + 1, pl.ds(64 * q, 64), :])
-        for c in moves:
-            c.wait_send()
-        if s < 2:
-            moves = exchange(s + 1)
-        if s == 0:
-            for k in range(SECOND, nx):
-                send_row(k)
-    for c in winds:
+            dst[bottom, :] = dst[bottom, :] + weight * (AL[pl.ds(0, 64, stride=32), :] * yin[n])
+            dst[top, :] = dst[top, :] - weight * (AH[pl.ds(31, 64, stride=32), :] * yin[n + 1])
+            if s < 2:
+                moves[q] = exchange(s + 1, q)
+                sent += moves[q]
+    for c in sent:
         c.wait_send()
     rest = pl.ds(8, 8 * (nx * ny - 1))
     whole = remote(recv_ref.at[rest, :], recv_ref.at[rest, :], a2a_send, a2a_recv, right)
@@ -517,13 +510,13 @@
         in_specs=[pl.BlockSpec(memory_space=pltpu.SMEM)] + [HB] * 8 + [VM] * 4,
         out_specs=[VM] * 3,
         scratch_shapes=[plane] * 5 + [pltpu.VMEM((8, 128, 128), f32)] * 3 + [pltpu.VMEM((1024, 256), f32), pltpu.VMEM((16, 128), f32)] + [block] * 5
-        + [pltpu.VMEM((N_CE * 8, 128), f32), pltpu.VMEM((1024, 768), bf16), pltpu.VMEM((8, 128), f32), pltpu.VMEM((8, 128), f32)]
+        + [pltpu.VMEM((N_CE * 8, 128), f32), pltpu.VMEM((1024, 512), bf16), pltpu.VMEM((8, 128), f32), pltpu.VMEM((8, 128), f32)]
         + [
             pltpu.VMEM((6, WX * WY, 128), f32), pltpu.VMEM((65 * 32, 128), f32), plane, plane, plane, plane,
             pltpu.VMEM((2, 32, 128), f32), pltpu.VMEM((64 * WY, 128), f32),
-            pltpu.VMEM((12, 32, 128), f32), pltpu.VMEM((6, 128, 128), f32), pltpu.VMEM((6, 128, 128), f32),
+            pltpu.VMEM((12, 32, 128), f32), pltpu.VMEM((12, 64, 128), f32), pltpu.VMEM((12, 64, 128), f32),
             pltpu.VMEM((2, 64, 128), f32), pltpu.VMEM((2, 64, 128), f32), pltpu.VMEM((1024, 512), bf16),
-            DMA, DMA, DMA((12,)), DMA((12,)), DMA((6,)), DMA((6,)), DMA((4,)), DMA((4,)), pltpu.SemaphoreType.REGULAR, DMA((8,)),
+            DMA, DMA, DMA((12,)), DMA((12,)), DMA((12,)), DMA((12,)), DMA((4,)), DMA((4,)), pltpu.SemaphoreType.REGULAR, DMA((8,)),
         ],
         compiler_params=pltpu.CompilerParams(vmem_limit_bytes=50 * 2**20, collective_id=0, has_side_effects=True),
         cost_estimate=pl.CostEstimate(flops=5_000_000_000, bytes_accessed=8_000_000, transcendentals=0),
@@ -535,16 +528,10 @@
     return lax.broadcasted_iota(jnp.int32, (n, n), 0) < lax.broadcasted_iota(jnp.int32, (n, n), 1)
 
 
-def split3(x):
-    hi = x.astype(jnp.bfloat16)
-    rest = x - hi.astype(f32)
-    mid = rest.astype(jnp.bfloat16)
-    return hi, mid, (rest - mid.astype(f32)).astype(jnp.bfloat16)
-
-
-def compact_kernel(recv_ref, ti_ref, vi_ref, to_ref, vo_ref, ro_ref, mo_ref, X):
-    to_ref[...] = ti_ref[...]
-    vo_ref[...] = vi_ref[...]
+def compact_kernel(recv_ref, ti_ref, vi_ref, to_ref, vo_ref, ro_ref, mo_ref, X, sems):
+    passing = [pltpu.make_async_copy(ti_ref, to_ref, sems.at[0]), pltpu.make_async_copy(vi_ref, vo_ref, sems.at[1])]
+    for c in passing:
+        c.start()
     rows = []
     for g in range(8):
         rows.append(recv_ref[pl.ds(g * 128, 128), 128:256].T[0:1])
@@ -560,15 +547,17 @@
     pos = jnp.concatenate(pos, axis=1).astype(jnp.int32)
     for g in range(8):
         at = pl.ds(g * 128, 128)
-        for k, part in enumerate(split3(recv_ref[at, :])):
+        for k, part in enumerate(split2(recv_ref[at, :])):
             X[at, k * 256:k * 256 + 256] = part
     for n in range(4):
         ids = lax.broadcasted_iota(jnp.int32, (128, 1024), 0) + n * 128
         hot = jnp.where(ids == pos, 1.0, 0.0).astype(jnp.bfloat16)
         d = jnp.dot(hot, X[...], preferred_element_type=f32)
-        d = d[:, 0:256] + (d[:, 256:512] + d[:, 512:768])
+        d = d[:, 0:256] + d[:, 256:512]
         ro_ref[pl.ds(n * 128, 128), :] = d[:, 0:128]
         mo_ref[pl.ds(n * 128, 128), :] = d[:, 128:256]
+    for c in passing:
+        c.wait()
 
 
 def compacted(recv, t, v):
@@ -578,8 +567,8 @@
     return pl.pallas_call(
         compact_kernel,
         out_shape=(field, field, drops, drops),
-        in_specs=[VM] * 3, out_specs=[VM] * 4,
-        scratch_shapes=[pltpu.VMEM((1024, 768), jnp.bfloat16)],
+        in_specs=[VM] * 3, out_specs=[pl.BlockSpec(memory_space=pltpu.HBM)] * 2 + [VM] * 2,
+        scratch_shapes=[pltpu.VMEM((1024, 512), jnp.bfloat16), pltpu.SemaphoreType.DMA((2,))],
         compiler_params=pltpu.CompilerParams(vmem_limit_bytes=12 * 2**20),
         cost_estimate=pl.CostEstimate(flops=800_000_000, bytes_accessed=2_000_000, transcendentals=0),
         name="compact",

time: 53.7 us -> 49.5 us (0.922)
  the two profiles are of different devices: /device:TPU:1 before, /device:TPU:0 now
where the time goes in v4:
time: 49.5 us; the launch traced here: 49 us
  Pallas kernels  47.7 us (96%)
  local copies, waits for them, and re-layouts  0.7 us (1%)
  between operations  0.67 us (1%)
    pallas_call x1, Pallas kernels, step_call(): pl.pallas_call(functools.partial(step_kernel, nx, ny), out_shape=(jax.Sha...  45.5 us
    pallas_call x1, Pallas kernels, compacted(): pl.pallas_call(compact_kernel, out_shape=(field, field, drops, drops), in...  2.14 us

profile of v4, /device:TPU:0, one launch (start us, length us, event | category | flops | bytes accessed | tf_op | source)
XLA Modules:
  0.0 49.0 jit_solution(4342753648993710223)
XLA Ops:
  0.6 0.0 copy-start.2
  0.6 0.0 copy-start.1
  0.7 0.0 copy-start
  0.7 0.7 %copy-done.2 = s32[1024]{0:T(1024)S(1)} copy-done((s32[1024]{0:T(1024)S(1)}, s32[1024]{0:T(1024)}, u32[]{:S(2)}) %copy-start.2) | copy-done | bytes 4120
  1.3 0.0 copy-done.1
  1.3 0.0 copy-done
  1.4 45.5 %step.1 = (f32[2048,128]{1,0:T(8,128)S(1)}, f32[2048,128]{1,0:T(8,128)S(1)}, f32[1024,256]{1,0:T(8,128)S(1)}) custom-call(s32[1024]{0:T(1024)S(1)} %copy-done, f32[2048,128]{1,0:T(8,128)} %bitcast.18, f32[2048,128]{1,0:T(8,128)} %bitcast.19, f32[2048,128]{1,0:T(8,128)} %bitcast.20, f32[2048,128]{1,0:T(8,128)} %bitcast.21, f32[2048,128]{1,0:T(8,128)} %bitcast.22, ...), custom_call_target="tpu_custom_call" | custom-call | flops 5000000000 | bytes 8000000 | tf_op jit(solution)/shard_map/step/pallas_call | solution.py:507
  46.9 2.1 %compact.1 = (f32[2048,128]{1,0:T(8,128)}, f32[2048,128]{1,0:T(8,128)}, f32[512,128]{1,0:T(8,128)}, f32[512,128]{1,0:T(8,128)}) custom-call(f32[1024,256]{1,0:T(8,128)S(1)} %get-tuple-element.11.recv_ref, f32[2048,128]{1,0:T(8,128)S(1)} %get-tuple-element.12.ti_ref, f32[2048,128]{1,0:T(8,128)S(1)} %get-tuple-element.13.vi_ref), custom_call_target="tpu_custom_call" | custom-call | flops 800000000 | bytes 2000000 | tf_op jit(solution)/shard_map/compact/pallas_call | solution.py:567
Async XLA Ops:
  0.6 0.7 %copy-start.2 = (s32[1024]{0:T(1024)S(1)}, s32[1024]{0:T(1024)}, u32[]{:S(2)}) copy-start(s32[1024]{0:T(1024)} %param.21) | copy-start | bytes 12292
  0.6 0.7 %copy-start.1 = (s32[1024]{0:T(1024)S(1)}, s32[1024]{0:T(1024)}, u32[]{:S(2)}) copy-start(s32[1024]{0:T(1024)} %param.19) | copy-start | bytes 12292
  0.7 0.7 %copy-start = (s32[1024]{0:T(1024)S(1)}, s32[1024]{0:T(1024)}, u32[]{:S(2)}) copy-start(s32[1024]{0:T(1024)} %index.1) | copy-start | bytes 12292

commit v5 on v4

--- a/solution.py
+++ b/solution.py
@@ -164,8 +164,7 @@
             cell[pl.ds(g, 1), :] = jnp.sum(picked, axis=0, keepdims=True)
 
 
-def condense_blocks(rad_ref, flo_ref, mul_ref, cnt_ref, heat_ref, R, S, C, F, M, ct_ref, cv_ref):
-
+def enter_blocks(rad_ref, flo_ref, mul_ref, R, F, M):
     def enter(g, c):
         to = pl.ds(g, 128, stride=8)
         R[to, :] = rad_ref[g].T
@@ -173,6 +172,9 @@
         M[to, :] = mul_ref[g].T
         return c
     lax.fori_loop(0, 8, enter, 0)
+
+
+def condense_blocks(cnt_ref, heat_ref, R, S, C, F, M, ct_ref, cv_ref):
     counts = cnt_ref[...]
     zero = jnp.zeros((8, 128), jnp.float32)
     U = 32
@@ -307,7 +309,7 @@
     upper, lower = (ix, mod(iy + 1, ny)), (ix, mod(iy - 1, ny))
 
     fetched = []
-    for n, (src, dst) in enumerate(((t_hbm, t_ref), (v_hbm, v_ref), (rad_hbm, rad_ref), (flo_hbm, flo_ref), (mul_hbm, mul_ref), (vv_hbm, vv_ref), (u_hbm, u_ref), (w_hbm, w_ref))):
+    for n, (src, dst) in enumerate(((rad_hbm, rad_ref), (flo_hbm, flo_ref), (mul_hbm, mul_ref), (t_hbm, t_ref), (v_hbm, v_ref), (vv_hbm, vv_ref), (u_hbm, u_ref), (w_hbm, w_ref))):
         fetched.append(pltpu.make_async_copy(src, dst, loads.at[n]))
         fetched[-1].start()
     barrier = pltpu.get_barrier_semaphore()
@@ -319,12 +321,13 @@
     def remote(src, dst, s, r, to):
         return pltpu.make_async_remote_copy(src_ref=src, dst_ref=dst, send_sem=s, recv_sem=r, device_id=to, device_id_type=MESH)
 
-    fetched[0].wait()
-    fetched[1].wait()
+    for n in (0, 1, 2):
+        fetched[n].wait()
+    enter_blocks(rad_ref, flo_ref, mul_ref, R, F, M)
+    fetched[3].wait()
+    fetched[4].wait()
     gather_cells(index, t_ref, v_ref, square_ref, ct_ref, cv_ref, S, C)
-    for n in (2, 3, 4):
-        fetched[n].wait()
-    condense_blocks(rad_ref, flo_ref, mul_ref, cnt_ref, heat_ref, R, S, C, F, M, ct_ref, cv_ref)
+    condense_blocks(cnt_ref, heat_ref, R, S, C, F, M, ct_ref, cv_ref)
     fetched[5].wait()
     fetched[6].wait()
     vout[0] = vv_ref[pl.ds(31, 64, stride=32), :]
@@ -344,32 +347,6 @@
     ]
     for c in winds:
         c.start()
-    zed = lax.rem(square_ref[...], 128).astype(f32).T.astype(jnp.int32)
-    heat = heat_ref[...].T
-    lanes = lax.broadcasted_iota(jnp.int32, (128, 128), 1)
-    for g in range(8):
-        level = lanes == zed[:, g:g + 1]
-        at = pl.ds(g * 128, 128)
-        for q in range(2):
-            h = jnp.where(level, heat[:, q * 8 + g:q * 8 + g + 1], 0.0)
-            hi, lo = split2(h)
-            W[at, q * 128:q * 128 + 128] = hi
-            W[at, 256 + q * 128:256 + q * 128 + 128] = lo
-    cells = lax.shift_right_logical(cell_ref[...], 7)
-
-    def scatter(k, c):
-        at = pl.multiple_of(k * 128, 128)
-        ids = lax.broadcasted_iota(jnp.int32, (128, 1024), 0) + at
-        hot = jnp.where(ids == cells, 1.0, 0.0).astype(jnp.bfloat16)
-        d = jnp.dot(hot, W[...], preferred_element_type=f32)
-        for q, ref in ((0, t_ref), (1, v_ref)):
-            add = d[:, q * 128:q * 128 + 128] + d[:, 256 + q * 128:256 + q * 128 + 128]
-            new = ref[pl.ds(at, 128), :] + add
-            for j in range(4):
-                E[q, pl.ds(pl.multiple_of((k * 4 + j + 1) * WY + 8, 8), 32), :] = new[j * 32:j * 32 + 32]
-        return c
-    lax.fori_loop(0, 16, scatter, 0)
-
     def plane(x):
         return x * WY + 8
 
@@ -388,8 +365,6 @@
             c.start()
         return moves
 
-    moves = [exchange(0, 0), exchange(0, 1)]
-    sent = [*winds, *moves[0], *moves[1]]
     collect_blocks(R, S, C, F, M, marks, X)
     moves_to = move_ref[...]
 
@@ -403,14 +378,47 @@
     def send_row(k):
         row_moves(nx, ny, ix, iy, k, send_ref, recv_ref, a2a_send, a2a_recv)
 
-    place(0)
+    order = sorted(range(nx), key=lambda k: -min(k, nx - k))
+    place(order[0])
     pl.semaphore_wait(rows, ny - 1)
-    send_row(0)
-    for k in range(1, nx):
+    send_row(order[0])
+    for n, k in enumerate(order[1:]):
         place(k)
-        send_row(k)
+        if n < 3:
+            send_row(k)
     mine = pl.ds(pl.multiple_of(me * 8, 8), 8)
     recv_ref[mine, :] = send_ref[mine, :]
+
+    zed = lax.rem(square_ref[...], 128).astype(f32).T.astype(jnp.int32)
+    heat = heat_ref[...].T
+    lanes = lax.broadcasted_iota(jnp.int32, (128, 128), 1)
+    for g in range(8):
+        level = lanes == zed[:, g:g + 1]
+        at = pl.ds(g * 128, 128)
+        for q in range(2):
+            h = jnp.where(level, heat[:, q * 8 + g:q * 8 + g + 1], 0.0)
+            hi, lo = split2(h)
+            W[at, q * 128:q * 128 + 128] = hi
+            W[at, 256 + q * 128:256 + q * 128 + 128] = lo
+    cells = lax.shift_right_logical(cell_ref[...], 7)
+
+    def scatter(k, c):
+        at = pl.multiple_of(k * 128, 128)
+        ids = lax.broadcasted_iota(jnp.int32, (128, 1024), 0) + at
+        hot = jnp.where(ids == cells, 1.0, 0.0).astype(jnp.bfloat16)
+        d = jnp.dot(hot, W[...], preferred_element_type=f32)
+        for q, ref in ((0, t_ref), (1, v_ref)):
+            add = d[:, q * 128:q * 128 + 128] + d[:, 256 + q * 128:256 + q * 128 + 128]
+            new = ref[pl.ds(at, 128), :] + add
+            for j in range(4):
+                E[q, pl.ds(pl.multiple_of((k * 4 + j + 1) * WY + 8, 8), 32), :] = new[j * 32:j * 32 + 32]
+        return c
+    lax.fori_loop(0, 16, scatter, 0)
+
+    moves = [exchange(0, 0), exchange(0, 1)]
+    sent = [*winds, *moves[0], *moves[1]]
+    send_row(order[4])
+    send_row(order[5])
 
     fetched[7].wait()
     for c in winds:
@@ -472,6 +480,8 @@
                 return f, low
             f0 = src[pl.ds(plane(1), 32), :]
             lax.fori_loop(0, 64 // UNROLL, step, (f0, AX[pl.ds(0, 32), :] * f0))
+            if s == 0:
+                send_row(order[6 + q])
             for c in moves[q]:
                 c.wait_recv()
             if s < 2:

time: 49.5 us -> 46 us (0.929)
  Pallas kernels: 47.7 us -> 44.5 us
    pallas_call x1, Pallas kernels: 45.5 us -> 42.4 us  [step_call(): pl.pallas_call(functools.partial(step_kernel, nx, ny), out_shape=(jax.Sha...]
where the time goes in v5:
time: 46 us; the launch traced here: 45.9 us
  Pallas kernels  44.5 us (97%)
  local copies, waits for them, and re-layouts  0.7 us (2%)
  between operations  0.67 us (1%)
    pallas_call x1, Pallas kernels, step_call(): pl.pallas_call(functools.partial(step_kernel, nx, ny), out_shape=(jax.Sha...  42.4 us
    pallas_call x1, Pallas kernels, compacted(): pl.pallas_call(compact_kernel, out_shape=(field, field, drops, drops), in...  2.14 us

profile of v5, /device:TPU:0, one launch (start us, length us, event | category | flops | bytes accessed | tf_op | source)
XLA Modules:
  0.0 45.9 jit_solution(1206910722012518622)
XLA Ops:
  0.6 0.0 copy-start.2
  0.6 0.0 copy-start.1
  0.7 0.0 copy-start
  0.7 0.7 %copy-done.2 = s32[1024]{0:T(1024)S(1)} copy-done((s32[1024]{0:T(1024)S(1)}, s32[1024]{0:T(1024)}, u32[]{:S(2)}) %copy-start.2) | copy-done | bytes 4120
  1.3 0.0 copy-done.1
  1.3 0.0 copy-done
  1.4 42.4 %step.1 = (f32[2048,128]{1,0:T(8,128)S(1)}, f32[2048,128]{1,0:T(8,128)S(1)}, f32[1024,256]{1,0:T(8,128)S(1)}) custom-call(s32[1024]{0:T(1024)S(1)} %copy-done, f32[2048,128]{1,0:T(8,128)} %bitcast.18, f32[2048,128]{1,0:T(8,128)} %bitcast.19, f32[2048,128]{1,0:T(8,128)} %bitcast.20, f32[2048,128]{1,0:T(8,128)} %bitcast.21, f32[2048,128]{1,0:T(8,128)} %bitcast.22, ...), custom_call_target="tpu_custom_call" | custom-call | flops 5000000000 | bytes 8000000 | tf_op jit(solution)/shard_map/step/pallas_call | solution.py:517
  43.8 2.1 %compact.1 = (f32[2048,128]{1,0:T(8,128)}, f32[2048,128]{1,0:T(8,128)}, f32[512,128]{1,0:T(8,128)}, f32[512,128]{1,0:T(8,128)}) custom-call(f32[1024,256]{1,0:T(8,128)S(1)} %get-tuple-element.11.recv_ref, f32[2048,128]{1,0:T(8,128)S(1)} %get-tuple-element.12.ti_ref, f32[2048,128]{1,0:T(8,128)S(1)} %get-tuple-element.13.vi_ref), custom_call_target="tpu_custom_call" | custom-call | flops 800000000 | bytes 2000000 | tf_op jit(solution)/shard_map/compact/pallas_call | solution.py:577
Async XLA Ops:
  0.6 0.7 %copy-start.2 = (s32[1024]{0:T(1024)S(1)}, s32[1024]{0:T(1024)}, u32[]{:S(2)}) copy-start(s32[1024]{0:T(1024)} %param.21) | copy-start | bytes 12292
  0.6 0.7 %copy-start.1 = (s32[1024]{0:T(1024)S(1)}, s32[1024]{0:T(1024)}, u32[]{:S(2)}) copy-start(s32[1024]{0:T(1024)} %param.19) | copy-start | bytes 12292
  0.7 0.7 %copy-start = (s32[1024]{0:T(1024)S(1)}, s32[1024]{0:T(1024)}, u32[]{:S(2)}) copy-start(s32[1024]{0:T(1024)} %index.1) | copy-start | bytes 12292

commit v6 on v5

--- a/solution.py
+++ b/solution.py
@@ -11,7 +11,7 @@
 f32 = jnp.float32
 SUBSTEPS = 6
 WX, WY = 66, 48
-UNROLL = 8
+UNROLL = 16
 
 clausius = 0.07
 growth = 200.0 / 3.0
@@ -148,13 +148,13 @@
 
 def gather_cells(index, t_ref, v_ref, cell_ref, ct, cv, T, V):
     def rows(k, c):
-        for j in range(16):
-            b = k * 16 + j
+        for j in range(32):
+            b = k * 32 + j
             at = lax.shift_right_logical(index[b], 7)
             T[pl.ds(b, 1), :] = t_ref[pl.ds(at, 1), :]
             V[pl.ds(b, 1), :] = v_ref[pl.ds(at, 1), :]
         return c
-    lax.fori_loop(0, 64, rows, 0)
+    lax.fori_loop(0, 32, rows, 0)
     level = lax.rem(cell_ref[...], 128)
     depth = lax.broadcasted_iota(jnp.int32, (128, 128), 0)
     for g in range(8):
@@ -438,8 +438,8 @@
     lax.fori_loop(0, 8, enter, 0)
 
     def faces(k, c):
-        for j in range(4):
-            x = k * 4 + j
+        for j in range(8):
+            x = k * 8 + j
             at = pl.ds(pl.multiple_of(x * 32, 32), 32)
             here = vv_ref[at, :]
             AL[at, :] = 0.25 * (here + VE[pl.ds(x * WY + 7, 32), :])
@@ -448,7 +448,7 @@
             AZ[at, :] = jnp.where(lane == 127, 0.0, 0.25 * (w + pltpu.roll(w, 127, 1)))
             AD[at, :] = jnp.where(lane == 0, 0.0, 0.25 * (w + pltpu.roll(w, 1, 1)))
         return c
-    lax.fori_loop(0, 16, faces, 0)
+    lax.fori_loop(0, 8, faces, 0)
 
     def face_x(k, c):
         for j in range(7):

time: 46 us -> 45.6 us (level)
    pallas_call x1, Pallas kernels: 42.4 us -> 41.9 us  [step_call(): pl.pallas_call(functools.partial(step_kernel, nx, ny), out_shape=(jax.Sha...]
where the time goes in v6:
time: 45.6 us; the launch traced here: 45.4 us
  Pallas kernels  44.1 us (97%)
  local copies, waits for them, and re-layouts  0.7 us (2%)
  between operations  0.67 us (1%)
    pallas_call x1, Pallas kernels, step_call(): pl.pallas_call(functools.partial(step_kernel, nx, ny), out_shape=(jax.Sha...  41.9 us
    pallas_call x1, Pallas kernels, compacted(): pl.pallas_call(compact_kernel, out_shape=(field, field, drops, drops), in...  2.14 us

profile of v6, /device:TPU:0, one launch (start us, length us, event | category | flops | bytes accessed | tf_op | source)
XLA Modules:
  0.0 45.4 jit_solution(10380386530724542450)
XLA Ops:
  0.6 0.0 copy-start.2
  0.6 0.0 copy-start.1
  0.7 0.0 copy-start
  0.7 0.7 %copy-done.2 = s32[1024]{0:T(1024)S(1)} copy-done((s32[1024]{0:T(1024)S(1)}, s32[1024]{0:T(1024)}, u32[]{:S(2)}) %copy-start.2) | copy-done | bytes 4120
  1.3 0.0 copy-done.1
  1.3 0.0 copy-done
  1.4 41.9 %step.1 = (f32[2048,128]{1,0:T(8,128)S(1)}, f32[2048,128]{1,0:T(8,128)S(1)}, f32[1024,256]{1,0:T(8,128)S(1)}) custom-call(s32[1024]{0:T(1024)S(1)} %copy-done, f32[2048,128]{1,0:T(8,128)} %bitcast.18, f32[2048,128]{1,0:T(8,128)} %bitcast.19, f32[2048,128]{1,0:T(8,128)} %bitcast.20, f32[2048,128]{1,0:T(8,128)} %bitcast.21, f32[2048,128]{1,0:T(8,128)} %bitcast.22, ...), custom_call_target="tpu_custom_call" | custom-call | flops 5000000000 | bytes 8000000 | tf_op jit(solution)/shard_map/step/pallas_call | solution.py:517
  43.3 2.1 %compact.1 = (f32[2048,128]{1,0:T(8,128)}, f32[2048,128]{1,0:T(8,128)}, f32[512,128]{1,0:T(8,128)}, f32[512,128]{1,0:T(8,128)}) custom-call(f32[1024,256]{1,0:T(8,128)S(1)} %get-tuple-element.11.recv_ref, f32[2048,128]{1,0:T(8,128)S(1)} %get-tuple-element.12.ti_ref, f32[2048,128]{1,0:T(8,128)S(1)} %get-tuple-element.13.vi_ref), custom_call_target="tpu_custom_call" | custom-call | flops 800000000 | bytes 2000000 | tf_op jit(solution)/shard_map/compact/pallas_call | solution.py:577
Async XLA Ops:
  0.6 0.7 %copy-start.2 = (s32[1024]{0:T(1024)S(1)}, s32[1024]{0:T(1024)}, u32[]{:S(2)}) copy-start(s32[1024]{0:T(1024)} %param.21) | copy-start | bytes 12292
  0.6 0.7 %copy-start.1 = (s32[1024]{0:T(1024)S(1)}, s32[1024]{0:T(1024)}, u32[]{:S(2)}) copy-start(s32[1024]{0:T(1024)} %param.19) | copy-start | bytes 12292
  0.7 0.7 %copy-start = (s32[1024]{0:T(1024)S(1)}, s32[1024]{0:T(1024)}, u32[]{:S(2)}) copy-start(s32[1024]{0:T(1024)} %index.1) | copy-start | bytes 12292
